TPU v7x, 128 devices: a whole 4x4x4 slice. The times are simulated.
128 devices in a mesh: dp: 1, tp: 2 (over core), sp: 64 (over z, y, x).
Axes of the slice: x: 4, y: 4, z: 4, core: 2. Of those that a mesh axis runs over, the one named last changes fastest.
Arguments:
- hidden: bfloat16 [2, 8192, 2048], P('dp', 'sp')
- bucket: int32 [2, 32, 8192], P('dp', 'tp', 'sp')
- w_qk: bfloat16 [2048, 32, 64], P(None, 'tp')
- w_v: bfloat16 [2048, 32, 64], P(None, 'tp')
- w_o: bfloat16 [32, 64, 2048], P('tp')
Outputs:
- output: bfloat16 [2, 8192, 2048], P('dp', 'sp', 'tp')
All inputs are finite; a program needn't handle non-finite values.
Results may differ from a plain program's by a relative error of at most 0.0144573.
Values are sent between devices in bfloat16 or wider.
A program may use at most 1 GiB of HBM per device.

v0:
```python
import jax
import jax.numpy as jnp
from jax import lax
from jax.sharding import PartitionSpec as P

CHUNK = 128
MASK_VALUE = -1e5


def unit_keys(qk_rows):
    wide_rows = qk_rows.astype(jnp.float32)
    return (wide_rows / jnp.sqrt(jnp.sum(wide_rows * wide_rows, axis=-1, keepdims=True))).astype(jnp.bfloat16)


def chunk_attention(q_rows, v_rows, halo_q, halo_v):
    num_batch, num_heads, tokens, head_dim = q_rows.shape
    block_shape = (num_batch, num_heads, tokens // CHUNK, CHUNK, head_dim)
    keys_cur = unit_keys(q_rows)
    keys_prev = jnp.concatenate([unit_keys(halo_q), keys_cur[:, :, : tokens - CHUNK]], axis=2)
    vals_prev = jnp.concatenate([halo_v, v_rows[:, :, : tokens - CHUNK]], axis=2)
    query_blk = q_rows.reshape(block_shape)
    score_scale = head_dim ** -0.5
    score_prev = jnp.einsum("bhncd,bhnkd->bhnck", query_blk, keys_prev.reshape(block_shape), preferred_element_type=jnp.float32) * score_scale
    score_cur = jnp.einsum("bhncd,bhnkd->bhnck", query_blk, keys_cur.reshape(block_shape), preferred_element_type=jnp.float32) * score_scale
    chunk_ids = jnp.arange(CHUNK)
    score_cur = jnp.where(chunk_ids[:, None] == chunk_ids[None, :], MASK_VALUE, score_cur)
    row_max = jnp.maximum(jnp.max(score_prev, axis=-1, keepdims=True), jnp.max(score_cur, axis=-1, keepdims=True))
    exp_prev = jnp.exp(score_prev - row_max)
    exp_cur = jnp.exp(score_cur - row_max)
    row_sum = jnp.sum(exp_prev, axis=-1, keepdims=True) + jnp.sum(exp_cur, axis=-1, keepdims=True)
    out_blk = jnp.einsum("bhnck,bhnkd->bhncd", (exp_prev / row_sum).astype(jnp.bfloat16), vals_prev.reshape(block_shape), preferred_element_type=jnp.float32)
    out_blk = out_blk + jnp.einsum("bhnck,bhnkd->bhncd", (exp_cur / row_sum).astype(jnp.bfloat16), v_rows.reshape(block_shape), preferred_element_type=jnp.float32)
    return out_blk.astype(jnp.bfloat16).reshape(num_batch, num_heads, tokens, head_dim)


def solution(mesh):
    group_size = mesh.shape["sp"]
    neighbour_pairs = [(source, (source + 1) % group_size) for source in range(group_size)]

    def local_step(hidden, bucket, w_qk, w_v, w_o):
        num_batch = hidden.shape[0]
        tok_dev = hidden.shape[1]
        num_heads = bucket.shape[1]
        head_dim = w_qk.shape[2]
        slot_cap = 2 * tok_dev // group_size
        n_buckets = group_size * tok_dev // CHUNK
        my_index = lax.axis_index("sp")
        w_both = jnp.concatenate([w_qk, w_v], axis=2)
        proj_rows = jnp.einsum("btd,dhe->bhte", hidden, w_both, preferred_element_type=jnp.float32).astype(jnp.bfloat16)
        local_pos = jnp.arange(tok_dev, dtype=jnp.int32)
        sort_order = jnp.argsort(bucket * tok_dev + local_pos, axis=-1)
        local_rank = jnp.argsort(sort_order, axis=-1)
        bucket_sorted = jnp.take_along_axis(bucket, sort_order, axis=-1)
        counts = jax.vmap(jax.vmap(lambda id_row: jnp.bincount(id_row, length=n_buckets)))(bucket).astype(jnp.int32)
        all_counts = lax.all_gather(counts, "sp")
        totals = jnp.sum(all_counts, axis=0)
        earlier = (jnp.arange(group_size) < my_index)[:, None, None, None]
        before_dev = jnp.sum(jnp.where(earlier, all_counts, 0), axis=0)
        offsets = jnp.cumsum(totals, axis=-1) - totals + before_dev - (jnp.cumsum(counts, axis=-1) - counts)
        sorted_target = jnp.take_along_axis(offsets, bucket_sorted, axis=-1) + local_pos
        dest_sorted = sorted_target // tok_dev
        dest_ids = jnp.arange(group_size, dtype=jnp.int32)
        send_start = jnp.sum(dest_sorted[:, :, None, :] < dest_ids[:, None], axis=-1, dtype=jnp.int32)
        send_end = jnp.sum(dest_sorted[:, :, None, :] <= dest_ids[:, None], axis=-1, dtype=jnp.int32)
        source_rank = send_start[..., None] + jnp.arange(slot_cap, dtype=jnp.int32)
        slot_valid = (source_rank < send_end[..., None]).reshape(num_batch, num_heads, group_size * slot_cap)
        source_rank = jnp.minimum(source_rank, tok_dev - 1).reshape(num_batch, num_heads, group_size * slot_cap)
        source_token = jnp.take_along_axis(sort_order, source_rank, axis=-1)
        send_rows = jnp.take_along_axis(proj_rows, source_token[..., None], axis=2)
        dest_base = jnp.repeat(dest_ids, slot_cap) * tok_dev
        send_target = jnp.where(slot_valid, jnp.take_along_axis(sorted_target, source_rank, axis=-1) - dest_base, tok_dev)
        recv_rows = lax.all_to_all(send_rows, "sp", 2, 2, tiled=True)
        recv_target = lax.all_to_all(send_target, "sp", 2, 2, tiled=True)
        slot_ids = jnp.arange(group_size * slot_cap, dtype=jnp.int32)
        inverse = jax.vmap(jax.vmap(lambda target_row: jnp.zeros(tok_dev, jnp.int32).at[target_row].set(slot_ids, mode="drop")))(recv_target)
        sorted_rows = jnp.take_along_axis(recv_rows, inverse[..., None], axis=2)
        halo_rows = lax.ppermute(sorted_rows[:, :, tok_dev - CHUNK:, :], "sp", neighbour_pairs)
        out_sorted = chunk_attention(sorted_rows[..., :head_dim], sorted_rows[..., head_dim:], halo_rows[..., :head_dim], halo_rows[..., head_dim:])
        back_rows = jnp.take_along_axis(out_sorted, jnp.minimum(recv_target, tok_dev - 1)[..., None], axis=2)
        returned = lax.all_to_all(back_rows, "sp", 2, 2, tiled=True)
        token_dest = jnp.take_along_axis(dest_sorted, local_rank, axis=-1)
        token_slot = token_dest * slot_cap + local_rank - jnp.take_along_axis(send_start, token_dest, axis=-1)
        attn_out = jnp.take_along_axis(returned, token_slot[..., None], axis=2)
        y_part = jnp.einsum("bhte,hed->btd", attn_out, w_o, preferred_element_type=jnp.float32)
        return lax.psum_scatter(y_part, "tp", scatter_dimension=2, tiled=True).astype(jnp.bfloat16)

    return jax.shard_map(local_step, mesh=mesh, in_specs=(P("dp", "sp", None), P("dp", "tp", "sp"), P(None, "tp", None), P(None, "tp", None), P("tp", None, None)), out_specs=P("dp", "sp", "tp"), check_vma=False)
```

profile of v0, /device:TPU:1, one launch (start us, length us, event | category | flops | bytes accessed | tf_op | source)
XLA Modules:
  0.0 917.6 jit_solution(5587907373768593793)
XLA Ops:
  10.1 28.8 %scatter_custom_fusion = s32[2048]{0:T(1024)S(1)} fusion(s32[4096]{0:T(1024)S(1)} %bitcast.145, s32[4096]{0:T(1024)S(1)} %broadcast.288, s32[]{:T(128)} %constant.71.clone.1), kind=kCustom, calls=%fused_computation.123 | custom fusion | flops 4096 | bytes 8196
  39.0 156.7 %all_gather.7 = s32[64,2,16,64]{3,2,1,0:T(8,128)S(1)} all-gather(s32[1,2,16,64]{3,2,1,0:T(8,128)S(1)} %all_gather.6), channel_id=1, replica_groups=mesh['dp'=1,'tp'=2,'sp'=64] {'sp'}, dimensions={0}, use_global_device_ids=true | all-gather | bytes 532480 | tf_op jit(solution)/shard_map/all_gather | solution.py:55
  196.9 5.9 fusion.12
  204.4 33.2 %gather_fusion.4 = s32[4096]{0:T(1024)S(1)} fusion(s32[2,16,128]{2,1,0:T(8,128)S(1)} %copy-done.2, s32[4096]{0:T(1024)S(1)} %bitcast.119), kind=kCustom, calls=%fused_computation.clone | custom fusion | bytes 81920 | tf_op jit(solution)/shard_map/jit(take_along_axis)/gather | solution.py:53
  237.7 34.4 %gather_fusion.5 = s32[4096]{0:T(1024)S(1)} fusion(s32[2,16,64]{2,1,0:T(8,128)S(1)} %subtract_subtract_fusion, s32[4096]{0:T(1024)S(1)} %bitcast.116), kind=kCustom, calls=%fused_computation.1.clone | custom fusion | bytes 81920 | tf_op jit(solution)/shard_map/jit(take_along_axis)/gather | solution.py:60
  273.6 65.8 %gather_fusion.8 = s32[8192]{0:T(1024)S(1)} fusion(s32[2,16,128]{2,1,0:T(8,128)S(1)} %get-tuple-element.23, s32[8192]{0:T(1024)S(1)} %bitcast.112), kind=kCustom, calls=%fused_computation.2.clone | custom fusion | bytes 163840 | tf_op jit(solution)/shard_map/jit(take_along_axis)/gather | solution.py:71
  339.7 65.8 %gather_fusion.9 = s32[8192]{0:T(1024)S(1)} fusion(s32[2,16,128]{2,1,0:T(8,128)S(1)} %copy-done.1, s32[8192]{0:T(1024)S(1)} %bitcast.113), kind=kCustom, calls=%fused_computation.5.clone | custom fusion | bytes 163840 | tf_op jit(solution)/shard_map/jit(take_along_axis)/gather | solution.py:68
  406.7 4.6 all-to-all-start
  411.6 88.8 %gather_fusion = bf16[8192,128]{1,0:T(8,128)(2,1)} fusion(bf16[2,16,128,128]{3,2,1,0:T(8,128)(2,1)S(1)} %copy.140, s32[8192]{0:T(1024)S(1)} %bitcast.111), kind=kCustom, calls=%fused_computation.6 | custom fusion | bytes 4292608 | tf_op jit(solution)/shard_map/jit(take_along_axis)/gather | solution.py:69
  500.4 7.5 copy_select_fusion.1
  507.9 10.2 %all-to-all-start.1 = ((bf16[2,16,256,128]{3,1,0,2:T(8,128)(2,1)}), bf16[2,16,256,128]{3,1,0,2:T(8,128)(2,1)}, u32[]{:S(2)}, u32[]{:S(2)}) async-start(bf16[2,16,256,128]{3,1,0,2:T(8,128)(2,1)} %copy_select_fusion.1), calls=%async_computation.1 | async-start | bytes 4194304 | tf_op jit(solution)/shard_map/all_to_all | solution.py:72
  520.6 30.5 %scatter_custom_fusion.1 = s32[4096]{0:T(1024)S(1)} fusion(s32[8192]{0:T(1024)S(1)} %bitcast.144, s32[8192]{0:T(1024)S(1)} %bitcast.143, s32[]{:T(128)} %constant.71.clone.1), kind=kCustom, calls=%fused_computation.120 | custom fusion | bytes 16388
  551.1 2.4 copy.142
  553.5 44.7 %gather_fusion.1 = bf16[4096,128]{1,0:T(8,128)(2,1)} fusion(bf16[2,16,256,128]{3,2,1,0:T(8,128)(2,1)S(1)} %copy.142, s32[4096]{0:T(1024)S(1)} %bitcast.115), kind=kCustom, calls=%fused_computation.7 | custom fusion | bytes 2146304 | tf_op jit(solution)/shard_map/jit(take_along_axis)/gather | solution.py:76
  598.2 1.6 copy.143
  602.0 17.1 %collective-permute-done = bf16[2,16,128,128]{2,3,1,0:T(8,128)(2,1)} collective-permute-done((bf16[2,16,128,128]{2,3,1,0:T(8,128)(2,1)S(1)}, bf16[2,16,128,128]{2,3,1,0:T(8,128)(2,1)}, u32[]{:S(2)}, u32[]{:S(2)}) %collective-permute-start) | collective-permute-done | bytes 1048608 | tf_op jit(solution)/shard_map/ppermute | solution.py:77
  620.3 1.6 multiply_reduce_fusion
  623.6 1.8 fusion.13
  625.8 88.8 %gather_fusion.2 = bf16[8192,64]{1,0:T(8,128)(2,1)} fusion(bf16[2,16,128,64]{3,2,1,0:T(8,128)(2,1)S(1)} %copy.146, s32[8192]{0:T(1024)S(1)} %bitcast.110), kind=kCustom, calls=%fused_computation.8 | custom fusion | bytes 2195456 | tf_op jit(solution)/shard_map/jit(take_along_axis)/gather | solution.py:79
  714.7 6.4 fusion.51
  721.1 2.3 reshape.328
  723.4 4.9 all-to-all-start.2
  729.1 12.4 %sort.32.cloned.1.call-done = (s32[2,16,128]{2,1,0:T(8,128)}, s32[2,16,128]{2,1,0:T(8,128)}) async-done(((s32[2,16,128]{2,1,0:T(8,128)}, s32[2,16,128]{2,1,0:T(8,128)}), (s32[2,16,128]{2,1,0:T(8,128)}, s32[2,16,128]{2,1,0:T(8,128)})) %sort.32.cloned.1.call-update) | async-done | bytes 32784 | tf_op jit(solution)/shard_map/jit(argsort)/sort | solution.py:52
  742.2 33.2 %gather_fusion.6 = s32[4096]{0:T(1024)S(1)} fusion(s32[2,16,128]{2,1,0:T(8,128)S(1)} %get-tuple-element.22, s32[4096]{0:T(1024)S(1)} %bitcast.118), kind=kCustom, calls=%fused_computation.3.clone | custom fusion | bytes 81920 | tf_op jit(solution)/shard_map/jit(take_along_axis)/gather | solution.py:81
  775.4 34.4 %gather_fusion.7 = s32[4096]{0:T(1024)S(1)} fusion(s32[2,16,64]{2,1,0:T(8,128)S(1)} %get-tuple-element.17, s32[4096]{0:T(1024)S(1)} %bitcast.117), kind=kCustom, calls=%fused_computation.4.clone | custom fusion | bytes 81920 | tf_op jit(solution)/shard_map/jit(take_along_axis)/gather | solution.py:82
  809.8 2.4 reshape.329
  812.2 2.4 copy.148
  814.6 44.7 %gather_fusion.3 = bf16[4096,64]{1,0:T(8,128)(2,1)} fusion(bf16[2,16,256,64]{3,2,1,0:T(8,128)(2,1)S(1)} %copy.148, s32[4096]{0:T(1024)S(1)} %bitcast.114), kind=kCustom, calls=%fused_computation.9 | custom fusion | bytes 1097728 | tf_op jit(solution)/shard_map/jit(take_along_axis)/gather | solution.py:83
  859.3 1.6 copy.149
  860.9 4.8 fusion.5
  865.8 43.2 %reduce-scatter.2.cloned.1.call-done = f32[2,128,1024]{2,1,0:T(8,128)} async-done(((f32[2,128,2048]{2,1,0:T(8,128)}), f32[2,128,1024]{2,1,0:T(8,128)}) %reduce-scatter.2.cloned.1.call-update) | async-done | bytes 1048592 | tf_op jit(solution)/shard_map/reduce_scatter | solution.py:85
  909.0 2.1 convert_element_type.50
  (105 shorter events, 19.2 us)
Async XLA Ops:
  6.5 190.3 %copy-start = (bf16[2,128,2048]{2,1,0:T(8,128)(2,1)S(1)}, bf16[2,128,2048]{2,1,0:T(8,128)(2,1)}, u32[]{:S(2)}) copy-start(bf16[2,128,2048]{2,1,0:T(8,128)(2,1)} %param.11) | copy-start | bytes 3145732
  6.5 197.1 %sort.30.cloned.1.call-start = ((), (), s32[]{:S(2)}) async-start(), calls=%async_computation.5 | async-start | bytes 98336 | tf_op jit(solution)/shard_map/jit(argsort)/sort | solution.py:51
  202.7 1.7 copy-start.2
  204.4 33.2 %copy-start.1 = (s32[2,16,128]{2,1,0:T(8,128)S(1)}, s32[2,16,128]{2,1,0:T(8,128)}, u32[]{:S(2)}) copy-start(s32[2,16,128]{2,1,0:T(8,128)} %get-tuple-element.10) | copy-start | bytes 49156
  406.7 101.2 %all-to-all-start = ((s32[64,1,128]{2,1,0:T(1,128)}), s32[64,1,128]{2,1,0:T(1,128)S(1)}, u32[]{:S(2)}, u32[]{:S(2)}) async-start(s32[64,1,128]{2,1,0:T(1,128)} %reshape.326), calls=%async_computation | async-start | bytes 65536 | tf_op jit(solution)/shard_map/all_to_all | solution.py:73
  507.9 12.0 %copy-start.5 = (s32[3]{0:T(128)S(1)}, s32[3]{0:T(128)}, u32[]{:S(2)}) copy-start(s32[3]{0:T(128)} %constant.126) | copy-start | bytes 40
  507.9 12.2 %copy-start.4 = (s32[3]{0:T(128)S(1)}, s32[3]{0:T(128)}, u32[]{:S(2)}) copy-start(s32[3]{0:T(128)} %constant.129) | copy-start | bytes 40
  507.9 43.2 %all-to-all-start.1 = ((bf16[2,16,256,128]{3,1,0,2:T(8,128)(2,1)}), bf16[2,16,256,128]{3,1,0,2:T(8,128)(2,1)}, u32[]{:S(2)}, u32[]{:S(2)}) async-start(bf16[2,16,256,128]{3,1,0,2:T(8,128)(2,1)} %copy_select_fusion.1), calls=%async_computation.1 | async-start | bytes 4194304 | tf_op jit(solution)/shard_map/all_to_all | solution.py:72
  599.9 19.1 %collective-permute-start = (bf16[2,16,128,128]{2,3,1,0:T(8,128)(2,1)S(1)}, bf16[2,16,128,128]{2,3,1,0:T(8,128)(2,1)}, u32[]{:S(2)}, u32[]{:S(2)}) collective-permute-start(bf16[2,16,128,128]{2,3,1,0:T(8,128)(2,1)S(1)} %broadcast_select_fusion), channel_id=1, source_target_pairs={{0,1},{1,2},{2,3},{3,4},{4,5},{5,6},{6,7},{7,8},{8,9},{9,10},{10,1... | collective-permute-start | bytes 3145736 | tf_op jit(solution)/shard_map/ppermute | solution.py:77
  723.4 86.4 %all-to-all-start.2 = ((bf16[64,2,4096]{2,1,0:T(2,128)(2,1)}), bf16[64,2,4096]{2,1,0:T(2,128)(2,1)S(1)}, u32[]{:S(2)}, u32[]{:S(2)}) async-start(bf16[64,2,4096]{2,1,0:T(2,128)(2,1)} %reshape.328), calls=%async_computation.2 | async-start | bytes 2097152 | tf_op jit(solution)/shard_map/all_to_all | solution.py:80
  728.3 13.2 %sort.32.cloned.1.call-start = ((), (), s32[]{:S(2)}) async-start(), calls=%async_computation.6 | async-start | bytes 98336 | tf_op jit(solution)/shard_map/jit(argsort)/sort | solution.py:52
  729.0 179.9 %reduce-scatter.2.cloned.1.call-start = ((), (), s32[]{:S(2)}) async-start(), calls=%async_computation.4 | async-start | bytes 3145728 | tf_op jit(solution)/shard_map/reduce_scatter | solution.py:85
  742.2 33.2 %copy-start.3 = (s32[2,16,128]{2,1,0:T(8,128)S(1)}, s32[2,16,128]{2,1,0:T(8,128)}, u32[]{:S(2)}) copy-start(s32[2,16,128]{2,1,0:T(8,128)} %get-tuple-element.11) | copy-start | bytes 49156
Sparse Core Ops, SparseCore 0:
  9.6 12.5 sort.34.cloned.1.call-done
  731.3 9.8 sort.36.cloned.1.call-done
  865.9 43.0 reduce-scatter.1
  (2 shorter events, 0.0 us)
where the time goes:
time: 919 us; the launch traced here: 918 us
  local copies, waits for them, and re-layouts  596 us (65%)
  blocking collectives  157 us (17%)
  waiting for transfers between devices  60.3 us (7%)
  other arithmetic  55 us (6%)
  starting transfers between devices  20.7 us (2%)
  matrix products  15.3 us (2%)
  between operations  13.8 us (2%)
    all_gather x1, blocking collectives, local_step(): all_counts = lax.all_gather(counts, 'sp')  157 us
    gather x1, local copies, waits for them, and re-layouts, local_step(): jnp.take_along_axis(out_sorted, jnp.minimum(recv_target, tok_dev - 1)[......  88.8 us
    gather x1, local copies, waits for them, and re-layouts, local_step(): send_rows = jnp.take_along_axis(proj_rows, source_token[..., None], axis=2)  88.8 us
    gather x2, local copies, waits for them, and re-layouts, local_step(): jnp.take_along_axis(sorted_target, source_rank, axis=-1) - dest_base  65.9 us
    gather x2, local copies, waits for them, and re-layouts, local_step(): source_token = jnp.take_along_axis(sort_order, source_rank, axis=-1)  65.9 us
    gather x2, local copies, waits for them, and re-layouts, local_step(): sorted_rows = jnp.take_along_axis(recv_rows, inverse[..., None], axis=2)  46.3 us
    gather x2, local copies, waits for them, and re-layouts, local_step(): attn_out = jnp.take_along_axis(returned, token_slot[..., None], axis=2)  46.3 us
    reduce_scatter x1, waiting for transfers between devices, local_step(): lax.psum_scatter(y_part, 'tp', scatter_dimension=2, tiled=True)  43.2 us
  transfers between devices with their start and end apart: 5, of which 2 were waited for; matrix products, arithmetic and copies ran while one was open for 22% of the time, Pallas kernels for 0%

commit v1 on v0

v1 whole, which is shorter than its diff:
```python
import functools

import jax
import jax.numpy as jnp
from jax import lax
from jax.experimental import pallas as pl
from jax.experimental.pallas import tpu as pltpu
from jax.sharding import PartitionSpec as P

CHIPS = 64
HALF = 32
TOK = 128
CHUNK = 128
HEADS = 16
DIM = 64
MODEL = 2048
SLOTS = 4
MASKED = -8e5
EXP_SCALE = 0.125 * 1.4426950408889634
F32 = jnp.float32
BF16 = jnp.bfloat16
NT = (((1,), (1,)), ((), ()))
TN = (((0,), (0,)), ((), ()))


def iota(shape, axis):
    return lax.broadcasted_iota(jnp.int32, shape, axis)


def one_hot(mask):
    return jnp.where(mask, 1.0, 0.0).astype(BF16)


def dot(a, b, dims=(((1,), (0,)), ((), ()))):
    return lax.dot_general(a, b, dims, preferred_element_type=F32)


def kernel(x_hbm, bucket_ref, wq_hbm, wv_hbm, wo_hbm, y_ref,
           x_buf, w_buf, wo_buf, b_send, b_recv, r_send, r_recv,
           first_rank, code_pair, code_quad, parity, slot_rank,
           slots, slots_out, keys, vals, qrows, back, back_out, o_send, o_recv, part_send, part_recv,
           load_sem, b_send_sem, b_recv_sem, r_send_sem, r_recv_sem, s_send_sem, s_recv_sem,
           k_send_sem, k_recv_sem, o_send_sem, o_recv_sem, p_send_sem, p_recv_sem):
    core = lax.axis_index("tp")
    chip = lax.axis_index("sp")
    other = 1 - core
    half = chip // HALF
    place = chip % HALF
    mine = core == half

    def peer(t, s):
        return {"dp": 0, "tp": t, "sp": s}

    def remote(src, dst, send, recv, t, s):
        return pltpu.make_async_remote_copy(
            src_ref=src, dst_ref=dst, send_sem=send, recv_sem=recv,
            device_id=peer(t, s), device_id_type=pl.DeviceIdType.MESH)

    barrier = pltpu.get_barrier_semaphore()

    def greet(s, _):
        for t in range(2):
            @pl.when((s != chip) | (core != t))
            def _():
                pl.semaphore_signal(barrier, inc=1, device_id=peer(t, s), device_id_type=pl.DeviceIdType.MESH)
        return 0

    lax.fori_loop(0, CHIPS, greet, 0)

    turn = (chip // 8) % 4
    x_load = pltpu.make_async_copy(x_hbm, x_buf, load_sem.at[0])
    x_load.start()

    def w_loads(step):
        group = (step + turn) % 4
        return (pltpu.make_async_copy(wq_hbm.at[pl.ds(group * 256, 256)], w_buf.at[step, 0], load_sem.at[1 + step]),
                pltpu.make_async_copy(wv_hbm.at[pl.ds(group * 256, 256)], w_buf.at[step, 1], load_sem.at[5 + step]))

    for step in range(4):
        for load in w_loads(step):
            load.start()
    wo_load = pltpu.make_async_copy(wo_hbm, wo_buf, load_sem.at[9])
    wo_load.start()

    for b in range(2):
        for h in range(HEADS):
            b_send[b * HEADS + h] = bucket_ref[b, h:h + 1, :]

    x_load.wait()

    def project(step):
        for load in w_loads(step):
            load.wait()
        group = (step + turn) % 4
        rows = dot(w_buf[step].reshape(512, MODEL), x_buf[...], NT).astype(BF16)
        for hh in range(4):
            for b in range(2):
                pair = b * HEADS + group * 4 + hh
                r_send[pair, 0:DIM] = rows[hh * DIM:(hh + 1) * DIM, b * TOK:(b + 1) * TOK]
                r_send[pair, DIM:2 * DIM] = rows[256 + hh * DIM:256 + (hh + 1) * DIM, b * TOK:(b + 1) * TOK]

    def send_rows(step):
        group = (step + turn) % 4

        def body(i, _):
            spot = (i + chip) % 8
            pair = (spot // 4) * HEADS + group * 4 + spot % 4
            target = core * HALF + pair

            @pl.when(target == chip)
            def _():
                @pl.when(mine)
                def _():
                    pltpu.make_async_copy(r_send.at[pair], r_recv.at[place], r_recv_sem.at[place]).start()

            @pl.when((target != chip) | jnp.logical_not(mine))
            def _():
                remote(r_send.at[pair], r_recv.at[place], r_send_sem, r_recv_sem.at[place], half, target).start()
            return 0

        lax.fori_loop(0, 8, body, 0)

    project(0)
    pl.semaphore_wait(barrier, 2 * CHIPS - 1)

    def send_buckets(i, _):
        pair = (i + place) % HALF
        target = core * HALF + pair
        for t in range(2):
            @pl.when((target == chip) & (core == t))
            def _():
                pltpu.make_async_copy(b_send.at[pair], b_recv.at[chip], b_recv_sem).start()

            @pl.when((target != chip) | (core != t))
            def _():
                remote(b_send.at[pair], b_recv.at[chip], b_send_sem, b_recv_sem, t, target).start()
        return 0

    lax.fori_loop(0, HALF, send_buckets, 0)
    send_rows(0)

    def project_more(step, _):
        project(step)
        send_rows(step)
        return 0

    lax.fori_loop(1, 4, project_more, 0)

    pltpu.make_async_copy(b_recv, b_recv, b_recv_sem).wait()
    lane256 = iota((TOK, 256), 1)
    count_mat = one_hot((lane256 >= TOK) | (iota((TOK, 256), 0) < lane256))
    ids = iota((8, CHIPS, TOK), 1)
    ids_f = ids.astype(F32)

    def rank_first(i, running):
        hot = jnp.where(b_recv[pl.ds(8 * i, 8)] == ids, 1.0, 0.0)
        counts = dot(hot.astype(BF16).reshape(512, TOK), count_mat)
        for a in range(8):
            block = counts[a * CHIPS:(a + 1) * CHIPS]
            first_rank[8 * i + a] = jnp.sum(hot[a] * (block[:, :TOK] + running), axis=0, keepdims=True)
            running = running + block[:, TOK:]
        return running

    totals = lax.fori_loop(0, 8, rank_first, jnp.zeros((CHIPS, TOK), F32))
    high = jnp.floor(totals * (1.0 / 64))
    low = totals - 64.0 * high
    below = one_hot(iota((CHIPS, CHIPS), 1) < iota((CHIPS, CHIPS), 0))
    offsets = 64.0 * dot(below, high.astype(BF16)) + dot(below, low.astype(BF16))
    shift = (core * HALF).astype(F32)
    within = iota((8, 1, TOK), 0)
    lane_id = iota((CHIPS, TOK), 1)

    def rank_second(i, chunk_counts):
        hot = jnp.where(b_recv[pl.ds(8 * i, 8)] == ids, 1.0, 0.0)
        rank = first_rank[pl.ds(8 * i, 8)] + jnp.sum(hot * offsets[None], axis=1, keepdims=True)
        chunk = jnp.floor(rank * (1.0 / CHUNK)) - shift
        chunk = jnp.where(chunk < 0.0, chunk + float(CHIPS), chunk)
        hot = jnp.where(chunk == ids_f, 1.0, 0.0)
        counts = dot(hot.astype(BF16).reshape(512, TOK), count_mat)
        slot = jnp.sum(hot * counts[:, :TOK].reshape(8, CHIPS, TOK), axis=1, keepdims=True)
        two = jnp.floor(chunk * 0.5)
        code_pair[pl.ds(8 * i, 8)] = chunk * 8.0 + slot + ((within % 2) * SLOTS).astype(F32)
        code_quad[pl.ds(8 * i, 8)] = two * 16.0 + slot + ((within % 4) * SLOTS).astype(F32)
        parity[pl.ds(8 * i, 8)] = chunk - 2.0 * two
        for a in range(8):
            spot = (8 * i + a + core * HALF) % CHIPS
            chunk_counts = chunk_counts + jnp.where(lane_id == spot, counts[a * CHIPS:(a + 1) * CHIPS, TOK:], 0.0)
        return chunk_counts

    chunk_counts = lax.fori_loop(0, 8, rank_second, jnp.zeros((CHIPS, TOK), F32)).astype(BF16)
    source = iota((TOK, 256), 1) // SLOTS
    sources = iota((TOK, 256), 0)
    base = dot(chunk_counts, one_hot(sources < source))
    filled = dot(chunk_counts, one_hot(sources == source))
    slot_no = (iota((CHIPS, 256), 1) % SLOTS).astype(F32)
    slot_rank[...] = jnp.where(slot_no < filled, base + slot_no, -1.0)

    owner_group = (chip % HEADS) // 4
    ids512 = iota((512, 256), 0).astype(F32)

    def share(quad):
        return remote(slots_out.at[:, quad], slots.at[:, 8 + quad], s_send_sem.at[quad], s_recv_sem.at[quad], other, chip)

    def to_slots(i, _):
        quad = 2 * ((owner_group + 8 - i // 2) % 4) + i % 2
        tiles = []
        for a in range(2):
            spot = quad * 4 + a * 2
            for n in range(2):
                pltpu.make_async_copy(r_recv.at[spot + n], r_recv.at[spot + n], r_recv_sem.at[spot + n]).wait()
            token = core * HALF + spot
            codes = jnp.concatenate([code_pair[token], code_pair[token + 1]], axis=1)
            rows = jnp.concatenate([r_recv[spot], r_recv[spot + 1]], axis=1)
            tiles.append(dot(one_hot(codes == ids512), rows, NT).reshape(CHIPS, 8, TOK))
        tile = jnp.concatenate(tiles, axis=1).astype(BF16)
        slots[1:1 + HALF, quad] = tile[:HALF]
        slots[0, quad] = tile[CHIPS - 1]
        slots_out[1:1 + HALF, quad] = tile[HALF:]
        slots_out[0, quad] = tile[HALF - 1]
        share(quad).start()
        return 0

    lax.fori_loop(0, 8, to_slots, 0)

    def share_wait(quad, _):
        share(quad).wait()
        return 0

    lax.fori_loop(0, 8, share_wait, 0)

    rank_ids = iota((CHUNK, 256), 0).astype(F32)

    def selector(u):
        return one_hot(slot_rank[pl.ds((u + CHIPS - 1) % CHIPS, 1), :] == rank_ids)

    def gather_chunk(u, _):
        rows = dot(selector(u), slots[u].reshape(256, TOK))
        q_wide = rows[:, :DIM]
        inverse = 1.0 / jnp.sqrt(jnp.sum(q_wide * q_wide, axis=1, keepdims=True))
        keys[u] = (q_wide * inverse).astype(BF16)
        qrows[u] = q_wide.astype(BF16)
        vals[u] = rows[:, DIM:].T.astype(BF16)
        return 0

    lax.fori_loop(0, HALF + 1, gather_chunk, 0)
    diagonal = iota((CHUNK, CHUNK), 0) == iota((CHUNK, CHUNK), 1)

    def back_share(n):
        return remote(back_out.at[:, pl.ds(4 * n, 4)], back.at[:, pl.ds(16 + 4 * n, 4)],
                      k_send_sem.at[n], k_recv_sem.at[n], other, chip)

    def attend(n, _):
        outs = []
        for a in range(2):
            u = 2 * n + a + 1
            q = qrows[u]
            before = dot(keys[u - 1], q, NT)
            now = jnp.where(diagonal, MASKED, dot(keys[u], q, NT))
            top = jnp.maximum(jnp.max(before, axis=0, keepdims=True), jnp.max(now, axis=0, keepdims=True))
            before = jnp.exp2((before - top) * EXP_SCALE)
            now = jnp.exp2((now - top) * EXP_SCALE)
            total = jnp.sum(before, axis=0, keepdims=True) + jnp.sum(now, axis=0, keepdims=True)
            inverse = 1.0 / total
            probs = jnp.concatenate([(before * inverse).astype(BF16), (now * inverse).astype(BF16)], axis=0)
            out = dot(jnp.concatenate([vals[u - 1], vals[u]], axis=1), probs).astype(BF16)
            outs.append(dot(out, selector(u)))
        tile = jnp.concatenate(outs, axis=0).T.astype(BF16).reshape(16, 16, TOK)
        back[:, n] = tile[:8]
        back_out[:, n] = tile[8:]

        @pl.when(n % 4 == 3)
        def _():
            back_share(n // 4).start()
        return 0

    lax.fori_loop(0, HALF // 2, attend, 0)

    def back_wait(n, _):
        back_share(n).wait()
        return 0

    lax.fori_loop(0, 4, back_wait, 0)

    ids_quad = iota((512, 512), 0).astype(F32)
    my_pair = place

    def to_tokens(i, _):
        quad = (i + place // 4) % 8
        token = core * HALF + quad * 4
        codes = jnp.concatenate([code_quad[token + a] for a in range(4)], axis=1)
        odd = jnp.concatenate([parity[token + a] for a in range(4)], axis=1)
        both = dot(back[quad].reshape(512, TOK), one_hot(codes == ids_quad), TN)
        rows = jnp.where(odd > 0.5, both[DIM:], both[:DIM]).astype(BF16)
        for a in range(4):
            o_send[quad * 4 + a] = rows[:, a * TOK:(a + 1) * TOK]
        for a in range(4):
            target = token + a

            @pl.when((target == chip) & mine)
            def _():
                pltpu.make_async_copy(o_send.at[quad * 4 + a], o_recv.at[my_pair], o_recv_sem).start()

            @pl.when((target != chip) | jnp.logical_not(mine))
            def _():
                remote(o_send.at[quad * 4 + a], o_recv.at[my_pair], o_send_sem, o_recv_sem, half, target).start()
        return 0

    lax.fori_loop(0, 8, to_tokens, 0)
    wo_load.wait()
    pltpu.make_async_copy(o_recv, o_recv, o_recv_sem).wait()

    def part_share(b):
        return remote(part_send.at[b], part_recv.at[b], p_send_sem.at[b], p_recv_sem.at[b], other, chip)

    def out_rows(b, side):
        lhs = o_recv[pl.ds(b * HEADS, HEADS)].reshape(HEADS * DIM, TOK)
        return dot(lhs, wo_buf[:, pl.ds(pl.multiple_of(side * 1024, 1024), 1024)], TN)

    for b in range(2):
        part_send[b] = out_rows(b, other)
        part_share(b).start()
    mine_parts = [out_rows(b, core) for b in range(2)]
    for b in range(2):
        part_share(b).wait()
        y_ref[b] = (mine_parts[b] + part_recv[b]).astype(BF16)

    @pl.when(mine)
    def _():
        pltpu.make_async_copy(b_recv.at[0:63], b_recv.at[0:63], b_send_sem).wait()
        pltpu.make_async_copy(r_send.at[0:31], r_send.at[0:31], r_send_sem).wait()
        pltpu.make_async_copy(o_send.at[0:31], o_send.at[0:31], o_send_sem).wait()

    @pl.when(jnp.logical_not(mine))
    def _():
        pltpu.make_async_copy(b_recv, b_recv, b_send_sem).wait()
        pltpu.make_async_copy(r_send, r_send, r_send_sem).wait()
        pltpu.make_async_copy(o_send, o_send, o_send_sem).wait()


def solution(mesh):
    def step(hidden, bucket, w_qk, w_v, w_o):
        x = hidden.reshape(2 * TOK, MODEL)
        wq = jnp.transpose(w_qk, (1, 2, 0)).reshape(HEADS * DIM, MODEL)
        wv = jnp.transpose(w_v, (1, 2, 0)).reshape(HEADS * DIM, MODEL)
        wo = w_o.reshape(HEADS * DIM, MODEL)
        any_spec = pl.BlockSpec(memory_space=pl.ANY)
        vmem_spec = pl.BlockSpec(memory_space=pltpu.VMEM)
        dma = pltpu.SemaphoreType.DMA
        return pl.pallas_call(
            kernel,
            out_shape=jax.ShapeDtypeStruct((2, TOK, MODEL // 2), BF16),
            in_specs=[any_spec, vmem_spec, any_spec, any_spec, any_spec],
            out_specs=vmem_spec,
            scratch_shapes=[
                pltpu.VMEM((2 * TOK, MODEL), BF16),
                pltpu.VMEM((4, 2, 256, MODEL), BF16),
                pltpu.VMEM((HEADS * DIM, MODEL), BF16),
                pltpu.VMEM((HALF, 1, TOK), jnp.int32),
                pltpu.VMEM((CHIPS, 1, TOK), jnp.int32),
                pltpu.VMEM((HALF, 2 * DIM, TOK), BF16),
                pltpu.VMEM((HALF, 2 * DIM, TOK), BF16),
                pltpu.VMEM((CHIPS, 1, TOK), F32),
                pltpu.VMEM((CHIPS, 1, TOK), F32),
                pltpu.VMEM((CHIPS, 1, TOK), F32),
                pltpu.VMEM((CHIPS, 1, TOK), F32),
                pltpu.VMEM((CHIPS, 256), F32),
                pltpu.VMEM((HALF + 1, 16, 16, TOK), BF16),
                pltpu.VMEM((HALF + 1, 8, 16, TOK), BF16),
                pltpu.VMEM((HALF + 1, CHUNK, DIM), BF16),
                pltpu.VMEM((HALF + 1, DIM, CHUNK), BF16),
                pltpu.VMEM((HALF + 1, CHUNK, DIM), BF16),
                pltpu.VMEM((8, HALF, 16, TOK), BF16),
                pltpu.VMEM((8, HALF // 2, 16, TOK), BF16),
                pltpu.VMEM((HALF, DIM, TOK), BF16),
                pltpu.VMEM((HALF, DIM, TOK), BF16),
                pltpu.VMEM((2, TOK, MODEL // 2), F32),
                pltpu.VMEM((2, TOK, MODEL // 2), F32),
                dma((10,)), dma(()), dma(()), dma(()), dma((HALF,)), dma((8,)), dma((8,)),
                dma((4,)), dma((4,)), dma(()), dma(()), dma((2,)), dma((2,)),
            ],
            compiler_params=pltpu.CompilerParams(collective_id=0, has_side_effects=True, vmem_limit_bytes=56 * 1024 * 1024),
            name="bucket_attention",
        )(x, bucket, wq, wv, wo)

    return jax.shard_map(
        step, mesh=mesh,
        in_specs=(P("dp", "sp", None), P("dp", "tp", "sp"), P(None, "tp", None), P(None, "tp", None), P("tp", None, None)),
        out_specs=P("dp", "sp", "tp"), check_vma=False)
```

time: 919 us -> 78.7 us (0.09)
  local copies, waits for them, and re-layouts: 596 us -> 1.87 us
  blocking collectives: 157 us -> 0 us
  Pallas kernels: 0 us -> 76.7 us
  waiting for transfers between devices: 60.3 us -> 0 us
  other arithmetic: 55 us -> 0 us
  starting transfers between devices: 20.7 us -> 0 us
  matrix products: 15.3 us -> 0 us
  between operations: 13.8 us -> 0.01 us
    gather x14 -> x0, local copies, waits for them, and re-layouts: 537 us -> none  [the longest x1 88.8 us: local_step(): jnp.take_along_axis(out_sorted, jnp.minimum(recv_target, tok_dev - 1)[......]
    all_gather x1 -> x0, blocking collectives: 157 us -> none  [local_step(): all_counts = lax.all_gather(counts, 'sp')]
    pallas_call x0 -> x1, Pallas kernels: none -> 76.7 us  [step(): pl.pallas_call(kernel, out_shape=jax.ShapeDtypeStruct((2, TOK, MODEL // 2...]
    reduce_scatter x1 -> x0, waiting for transfers between devices: 43.2 us -> none  [local_step(): lax.psum_scatter(y_part, 'tp', scatter_dimension=2, tiled=True)]
    unnamed x8 -> x0, other arithmetic: 36.9 us -> none
    unnamed x33 -> x1, local copies, waits for them, and re-layouts: 37.2 us -> 1.87 us
    all_to_all x3 -> x0, starting transfers between devices: 19.6 us -> none  [the longest x1 10.2 us: local_step(): recv_rows = lax.all_to_all(send_rows, 'sp', 2, 2, tiled=True)]
    ppermute x1 -> x0, waiting for transfers between devices: 17.1 us -> none  [local_step(): lax.ppermute(sorted_rows[:, :, tok_dev - CHUNK:, :], 'sp', neighbour_pairs)]
  transfers between devices with their start and end apart: 5 -> 0, of which waited for: 2 -> 0; matrix products, arithmetic and copies ran while one was open for 22% -> 0% of each run, Pallas kernels for 0% -> 0%
where the time goes in v1:
time: 78.7 us; the launch traced here: 78.5 us
  Pallas kernels  76.7 us (97%)
  local copies, waits for them, and re-layouts  1.87 us (2%)
    pallas_call x1, Pallas kernels, step(): pl.pallas_call(kernel, out_shape=jax.ShapeDtypeStruct((2, TOK, MODEL // 2...  76.7 us
    unnamed x1, local copies, waits for them, and re-layouts  1.87 us

profile of v1, /device:TPU:1, one launch (start us, length us, event | category | flops | bytes accessed | tf_op | source)
XLA Modules:
  0.0 78.5 jit_solution(2862340430891553285)
XLA Ops:
  0.0 76.7 %bucket_attention.1 = bf16[2,128,1024]{2,1,0:T(8,128)(2,1)} custom-call(bf16[256,2048]{1,0:T(8,128)(2,1)} %bitcast.11, s32[2,16,128]{2,1,0:T(8,128)} %bucket_ref.1, bf16[1024,2048]{1,0:T(8,128)(2,1)} %bitcast.8, bf16[1024,2048]{1,0:T(8,128)(2,1)} %bitcast.9, bf16[1024,2048]{1,0:T(8,128)(2,1)} %bitcast.10), custom_call_target="tpu_custom_call" | custom-call | tf_op jit(solution)/shard_map/bucket_attention/pallas_call | solution.py:349
  76.7 1.9 %copy.7 = bf16[2,128,1024]{2,1,0:T(8,128)(2,1)} copy(bf16[2,128,1024]{2,1,0:T(8,128)(2,1)} %bucket_attention.1) | data formatting | bytes 1048576

commit v2 on v1

--- a/solution.py
+++ b/solution.py
@@ -38,7 +38,7 @@
 def kernel(x_hbm, bucket_ref, wq_hbm, wv_hbm, wo_hbm, y_ref,
            x_buf, w_buf, wo_buf, b_send, b_recv, r_send, r_recv,
            first_rank, code_pair, code_quad, parity, slot_rank,
-           slots, slots_out, keys, vals, qrows, back, back_out, o_send, o_recv, part_send, part_recv,
+           slots, slots_out, picks, keys, vals, qrows, back, back_out, o_send, o_recv, part_send, part_recv,
            load_sem, b_send_sem, b_recv_sem, r_send_sem, r_recv_sem, s_send_sem, s_recv_sem,
            k_send_sem, k_recv_sem, o_send_sem, o_recv_sem, p_send_sem, p_recv_sem):
     core = lax.axis_index("tp")
@@ -56,17 +56,6 @@
             src_ref=src, dst_ref=dst, send_sem=send, recv_sem=recv,
             device_id=peer(t, s), device_id_type=pl.DeviceIdType.MESH)
 
-    barrier = pltpu.get_barrier_semaphore()
-
-    def greet(s, _):
-        for t in range(2):
-            @pl.when((s != chip) | (core != t))
-            def _():
-                pl.semaphore_signal(barrier, inc=1, device_id=peer(t, s), device_id_type=pl.DeviceIdType.MESH)
-        return 0
-
-    lax.fori_loop(0, CHIPS, greet, 0)
-
     turn = (chip // 8) % 4
     x_load = pltpu.make_async_copy(x_hbm, x_buf, load_sem.at[0])
     x_load.start()
@@ -81,6 +70,17 @@
             load.start()
     wo_load = pltpu.make_async_copy(wo_hbm, wo_buf, load_sem.at[9])
     wo_load.start()
+
+    barrier = pltpu.get_barrier_semaphore()
+
+    def greet(s, _):
+        for t in range(2):
+            @pl.when((s != chip) | (core != t))
+            def _():
+                pl.semaphore_signal(barrier, inc=1, device_id=peer(t, s), device_id_type=pl.DeviceIdType.MESH)
+        return 0
+
+    lax.fori_loop(0, CHIPS, greet, 0)
 
     for b in range(2):
         for h in range(HEADS):
@@ -230,50 +230,53 @@
 
     rank_ids = iota((CHUNK, 256), 0).astype(F32)
 
-    def selector(u):
-        return one_hot(slot_rank[pl.ds((u + CHIPS - 1) % CHIPS, 1), :] == rank_ids)
-
-    def gather_chunk(u, _):
-        rows = dot(selector(u), slots[u].reshape(256, TOK))
-        q_wide = rows[:, :DIM]
-        inverse = 1.0 / jnp.sqrt(jnp.sum(q_wide * q_wide, axis=1, keepdims=True))
-        keys[u] = (q_wide * inverse).astype(BF16)
-        qrows[u] = q_wide.astype(BF16)
-        vals[u] = rows[:, DIM:].T.astype(BF16)
-        return 0
-
-    lax.fori_loop(0, HALF + 1, gather_chunk, 0)
+    def gather_chunks(i, _):
+        spots = [3 * i + a for a in range(3)]
+        chosen = [one_hot(slot_rank[pl.ds((u + CHIPS - 1) % CHIPS, 1), :] == rank_ids) for u in spots]
+        found = [dot(pick, slots[u].reshape(256, TOK)) for u, pick in zip(spots, chosen)]
+        for u, pick in zip(spots, chosen):
+            picks[u] = pick
+        for u, rows in zip(spots, found):
+            q_wide = rows[:, :DIM]
+            inverse = 1.0 / jnp.sqrt(jnp.sum(q_wide * q_wide, axis=1, keepdims=True))
+            keys[u] = (q_wide * inverse).astype(BF16)
+            qrows[u] = q_wide.astype(BF16)
+            vals[u] = rows[:, DIM:].T.astype(BF16)
+        return 0
+
+    lax.fori_loop(0, (HALF + 1) // 3, gather_chunks, 0)
     diagonal = iota((CHUNK, CHUNK), 0) == iota((CHUNK, CHUNK), 1)
 
     def back_share(n):
         return remote(back_out.at[:, pl.ds(4 * n, 4)], back.at[:, pl.ds(16 + 4 * n, 4)],
                       k_send_sem.at[n], k_recv_sem.at[n], other, chip)
 
+    def softmax(before, now):
+        now = jnp.where(diagonal, MASKED, now)
+        top = jnp.maximum(jnp.max(before, axis=0, keepdims=True), jnp.max(now, axis=0, keepdims=True))
+        before = jnp.exp2((before - top) * EXP_SCALE)
+        now = jnp.exp2((now - top) * EXP_SCALE)
+        total = jnp.sum(before, axis=0, keepdims=True) + jnp.sum(now, axis=0, keepdims=True)
+        inverse = 1.0 / total
+        return jnp.concatenate([(before * inverse).astype(BF16), (now * inverse).astype(BF16)], axis=0)
+
     def attend(n, _):
-        outs = []
-        for a in range(2):
-            u = 2 * n + a + 1
-            q = qrows[u]
-            before = dot(keys[u - 1], q, NT)
-            now = jnp.where(diagonal, MASKED, dot(keys[u], q, NT))
-            top = jnp.maximum(jnp.max(before, axis=0, keepdims=True), jnp.max(now, axis=0, keepdims=True))
-            before = jnp.exp2((before - top) * EXP_SCALE)
-            now = jnp.exp2((now - top) * EXP_SCALE)
-            total = jnp.sum(before, axis=0, keepdims=True) + jnp.sum(now, axis=0, keepdims=True)
-            inverse = 1.0 / total
-            probs = jnp.concatenate([(before * inverse).astype(BF16), (now * inverse).astype(BF16)], axis=0)
-            out = dot(jnp.concatenate([vals[u - 1], vals[u]], axis=1), probs).astype(BF16)
-            outs.append(dot(out, selector(u)))
-        tile = jnp.concatenate(outs, axis=0).T.astype(BF16).reshape(16, 16, TOK)
-        back[:, n] = tile[:8]
-        back_out[:, n] = tile[8:]
-
-        @pl.when(n % 4 == 3)
+        spots = [4 * n + a + 1 for a in range(4)]
+        scores = [(dot(keys[u - 1], qrows[u], NT), dot(keys[u], qrows[u], NT)) for u in spots]
+        probs = [softmax(*pair) for pair in scores]
+        outs = [dot(jnp.concatenate([vals[u - 1], vals[u]], axis=1), p).astype(BF16) for u, p in zip(spots, probs)]
+        spread = [dot(o, picks[u]) for u, o in zip(spots, outs)]
+        for m in range(2):
+            tile = jnp.concatenate(spread[2 * m:2 * m + 2], axis=0).T.astype(BF16).reshape(16, 16, TOK)
+            back[:, 2 * n + m] = tile[:8]
+            back_out[:, 2 * n + m] = tile[8:]
+
+        @pl.when(n % 2 == 1)
         def _():
-            back_share(n // 4).start()
-        return 0
-
-    lax.fori_loop(0, HALF // 2, attend, 0)
+            back_share(n // 2).start()
+        return 0
+
+    lax.fori_loop(0, HALF // 4, attend, 0)
 
     def back_wait(n, _):
         back_share(n).wait()
@@ -366,6 +369,7 @@
                 pltpu.VMEM((CHIPS, 256), F32),
                 pltpu.VMEM((HALF + 1, 16, 16, TOK), BF16),
                 pltpu.VMEM((HALF + 1, 8, 16, TOK), BF16),
+                pltpu.VMEM((HALF + 1, CHUNK, 256), BF16),
                 pltpu.VMEM((HALF + 1, CHUNK, DIM), BF16),
                 pltpu.VMEM((HALF + 1, DIM, CHUNK), BF16),
                 pltpu.VMEM((HALF + 1, CHUNK, DIM), BF16),

time: 78.7 us -> 64.2 us (0.82)
  Pallas kernels: 76.7 us -> 62.1 us
    pallas_call x1, Pallas kernels: 76.7 us -> 62.1 us  [step(): pl.pallas_call(kernel, out_shape=jax.ShapeDtypeStruct((2, TOK, MODEL // 2...]
where the time goes in v2:
time: 64.2 us; the launch traced here: 64 us
  Pallas kernels  62.1 us (97%)
  local copies, waits for them, and re-layouts  1.87 us (3%)
    pallas_call x1, Pallas kernels, step(): pl.pallas_call(kernel, out_shape=jax.ShapeDtypeStruct((2, TOK, MODEL // 2...  62.1 us
    unnamed x1, local copies, waits for them, and re-layouts  1.87 us

profile of v2, /device:TPU:1, one launch (start us, length us, event | category | flops | bytes accessed | tf_op | source)
XLA Modules:
  0.0 64.0 jit_solution(13653627156333074498)
XLA Ops:
  0.0 62.1 %bucket_attention.1 = bf16[2,128,1024]{2,1,0:T(8,128)(2,1)} custom-call(bf16[256,2048]{1,0:T(8,128)(2,1)} %bitcast.11, s32[2,16,128]{2,1,0:T(8,128)} %bucket_ref.1, bf16[1024,2048]{1,0:T(8,128)(2,1)} %bitcast.8, bf16[1024,2048]{1,0:T(8,128)(2,1)} %bitcast.9, bf16[1024,2048]{1,0:T(8,128)(2,1)} %bitcast.10), custom_call_target="tpu_custom_call" | custom-call | tf_op jit(solution)/shard_map/bucket_attention/pallas_call | solution.py:352
  62.1 1.9 %copy.7 = bf16[2,128,1024]{2,1,0:T(8,128)(2,1)} copy(bf16[2,128,1024]{2,1,0:T(8,128)(2,1)} %bucket_attention.1) | data formatting | bytes 1048576

commit v3 on v2

--- a/solution.py
+++ b/solution.py
@@ -38,7 +38,7 @@
 def kernel(x_hbm, bucket_ref, wq_hbm, wv_hbm, wo_hbm, y_ref,
            x_buf, w_buf, wo_buf, b_send, b_recv, r_send, r_recv,
            first_rank, code_pair, code_quad, parity, slot_rank,
-           slots, slots_out, picks, keys, vals, qrows, back, back_out, o_send, o_recv, part_send, part_recv,
+           slots, slots_out, picks, keys, vals, qrows, back, back_out, o_send, o_recv, acc, part_recv,
            load_sem, b_send_sem, b_recv_sem, r_send_sem, r_recv_sem, s_send_sem, s_recv_sem,
            k_send_sem, k_recv_sem, o_send_sem, o_recv_sem, p_send_sem, p_recv_sem):
     core = lax.axis_index("tp")
@@ -68,8 +68,9 @@
     for step in range(4):
         for load in w_loads(step):
             load.start()
-    wo_load = pltpu.make_async_copy(wo_hbm, wo_buf, load_sem.at[9])
-    wo_load.start()
+    wo_loads = [pltpu.make_async_copy(wo_hbm.at[g], wo_buf.at[g], load_sem.at[9 + g]) for g in range(4)]
+    for load in wo_loads:
+        load.start()
 
     barrier = pltpu.get_barrier_semaphore()
 
@@ -103,15 +104,13 @@
         group = (step + turn) % 4
 
         def body(i, _):
-            spot = (i + chip) % 8
+            spot = (i + chip // 4 + chip // 16) % 8
             pair = (spot // 4) * HEADS + group * 4 + spot % 4
-            target = core * HALF + pair
-
-            @pl.when(target == chip)
-            def _():
-                @pl.when(mine)
-                def _():
-                    pltpu.make_async_copy(r_send.at[pair], r_recv.at[place], r_recv_sem.at[place]).start()
+            target = core * HALF + (spot // 4) * HEADS + (spot % 4) * 4 + group
+
+            @pl.when((target == chip) & mine)
+            def _():
+                pltpu.make_async_copy(r_send.at[pair], r_recv.at[place], r_recv_sem.at[place]).start()
 
             @pl.when((target != chip) | jnp.logical_not(mine))
             def _():
@@ -120,12 +119,10 @@
 
         lax.fori_loop(0, 8, body, 0)
 
-    project(0)
-    pl.semaphore_wait(barrier, 2 * CHIPS - 1)
-
     def send_buckets(i, _):
-        pair = (i + place) % HALF
-        target = core * HALF + pair
+        spot = (i + place) % HALF
+        pair = (spot // HEADS) * HEADS + (spot % 4) * 4 + (spot // 4) % 4
+        target = core * HALF + spot
         for t in range(2):
             @pl.when((target == chip) & (core == t))
             def _():
@@ -136,15 +133,20 @@
                 remote(b_send.at[pair], b_recv.at[chip], b_send_sem, b_recv_sem, t, target).start()
         return 0
 
+    project(0)
+    project(1)
+    acc[...] = jnp.zeros_like(acc)
+    pl.semaphore_wait(barrier, 2 * CHIPS - 1)
     lax.fori_loop(0, HALF, send_buckets, 0)
     send_rows(0)
+    send_rows(1)
 
     def project_more(step, _):
         project(step)
         send_rows(step)
         return 0
 
-    lax.fori_loop(1, 4, project_more, 0)
+    lax.fori_loop(2, 4, project_more, 0)
 
     pltpu.make_async_copy(b_recv, b_recv, b_recv_sem).wait()
     lane256 = iota((TOK, 256), 1)
@@ -195,7 +197,7 @@
     slot_no = (iota((CHIPS, 256), 1) % SLOTS).astype(F32)
     slot_rank[...] = jnp.where(slot_no < filled, base + slot_no, -1.0)
 
-    owner_group = (chip % HEADS) // 4
+    owner_group = chip % 4
     ids512 = iota((512, 256), 0).astype(F32)
 
     def share(quad):
@@ -231,7 +233,7 @@
     rank_ids = iota((CHUNK, 256), 0).astype(F32)
 
     def gather_chunks(i, _):
-        spots = [3 * i + a for a in range(3)]
+        spots = [11 * i + a for a in range(11)]
         chosen = [one_hot(slot_rank[pl.ds((u + CHIPS - 1) % CHIPS, 1), :] == rank_ids) for u in spots]
         found = [dot(pick, slots[u].reshape(256, TOK)) for u, pick in zip(spots, chosen)]
         for u, pick in zip(spots, chosen):
@@ -244,15 +246,15 @@
             vals[u] = rows[:, DIM:].T.astype(BF16)
         return 0
 
-    lax.fori_loop(0, (HALF + 1) // 3, gather_chunks, 0)
+    lax.fori_loop(0, (HALF + 1) // 11, gather_chunks, 0)
     diagonal = iota((CHUNK, CHUNK), 0) == iota((CHUNK, CHUNK), 1)
 
     def back_share(n):
         return remote(back_out.at[:, pl.ds(4 * n, 4)], back.at[:, pl.ds(16 + 4 * n, 4)],
                       k_send_sem.at[n], k_recv_sem.at[n], other, chip)
 
-    def softmax(before, now):
-        now = jnp.where(diagonal, MASKED, now)
+    def softmax(both):
+        before, now = both[:CHUNK], jnp.where(diagonal, MASKED, both[CHUNK:])
         top = jnp.maximum(jnp.max(before, axis=0, keepdims=True), jnp.max(now, axis=0, keepdims=True))
         before = jnp.exp2((before - top) * EXP_SCALE)
         now = jnp.exp2((now - top) * EXP_SCALE)
@@ -261,22 +263,20 @@
         return jnp.concatenate([(before * inverse).astype(BF16), (now * inverse).astype(BF16)], axis=0)
 
     def attend(n, _):
-        spots = [4 * n + a + 1 for a in range(4)]
-        scores = [(dot(keys[u - 1], qrows[u], NT), dot(keys[u], qrows[u], NT)) for u in spots]
-        probs = [softmax(*pair) for pair in scores]
+        spots = [8 * n + a + 1 for a in range(8)]
+        scores = [dot(keys[pl.ds(u - 1, 2)].reshape(2 * CHUNK, DIM), qrows[u], NT) for u in spots]
+        probs = [softmax(both) for both in scores]
         outs = [dot(jnp.concatenate([vals[u - 1], vals[u]], axis=1), p).astype(BF16) for u, p in zip(spots, probs)]
         spread = [dot(o, picks[u]) for u, o in zip(spots, outs)]
-        for m in range(2):
+        for m in range(4):
             tile = jnp.concatenate(spread[2 * m:2 * m + 2], axis=0).T.astype(BF16).reshape(16, 16, TOK)
-            back[:, 2 * n + m] = tile[:8]
-            back_out[:, 2 * n + m] = tile[8:]
-
-        @pl.when(n % 2 == 1)
-        def _():
-            back_share(n // 2).start()
-        return 0
-
-    lax.fori_loop(0, HALF // 4, attend, 0)
+            back[:, 4 * n + m] = tile[:8]
+            back_out[:, 4 * n + m] = tile[8:]
+
+        back_share(n).start()
+        return 0
+
+    lax.fori_loop(0, HALF // 8, attend, 0)
 
     def back_wait(n, _):
         back_share(n).wait()
@@ -285,10 +285,11 @@
     lax.fori_loop(0, 4, back_wait, 0)
 
     ids_quad = iota((512, 512), 0).astype(F32)
-    my_pair = place
+    my_batch = place // HEADS
+    my_pair = my_batch * HEADS + (chip % 4) * 4 + (chip // 4) % 4
 
     def to_tokens(i, _):
-        quad = (i + place // 4) % 8
+        quad = (((i // 4) + my_batch) % 2) * 4 + (i + chip) % 4
         token = core * HALF + quad * 4
         codes = jnp.concatenate([code_quad[token + a] for a in range(4)], axis=1)
         odd = jnp.concatenate([parity[token + a] for a in range(4)], axis=1)
@@ -296,36 +297,52 @@
         rows = jnp.where(odd > 0.5, both[DIM:], both[:DIM]).astype(BF16)
         for a in range(4):
             o_send[quad * 4 + a] = rows[:, a * TOK:(a + 1) * TOK]
-        for a in range(4):
+        for n in range(4):
+            a = (n + chip // 4 + chip // 16) % 4
             target = token + a
 
             @pl.when((target == chip) & mine)
             def _():
-                pltpu.make_async_copy(o_send.at[quad * 4 + a], o_recv.at[my_pair], o_recv_sem).start()
+                pltpu.make_async_copy(o_send.at[quad * 4 + a], o_recv.at[my_pair], o_recv_sem.at[my_pair]).start()
 
             @pl.when((target != chip) | jnp.logical_not(mine))
             def _():
-                remote(o_send.at[quad * 4 + a], o_recv.at[my_pair], o_send_sem, o_recv_sem, half, target).start()
+                remote(o_send.at[quad * 4 + a], o_recv.at[my_pair], o_send_sem, o_recv_sem.at[my_pair], half, target).start()
         return 0
 
     lax.fori_loop(0, 8, to_tokens, 0)
-    wo_load.wait()
-    pltpu.make_async_copy(o_recv, o_recv, o_recv_sem).wait()
+    for load in wo_loads:
+        load.wait()
 
     def part_share(b):
-        return remote(part_send.at[b], part_recv.at[b], p_send_sem.at[b], p_recv_sem.at[b], other, chip)
-
-    def out_rows(b, side):
-        lhs = o_recv[pl.ds(b * HEADS, HEADS)].reshape(HEADS * DIM, TOK)
-        return dot(lhs, wo_buf[:, pl.ds(pl.multiple_of(side * 1024, 1024), 1024)], TN)
-
-    for b in range(2):
-        part_send[b] = out_rows(b, other)
-        part_share(b).start()
-    mine_parts = [out_rows(b, core) for b in range(2)]
-    for b in range(2):
+        return remote(acc.at[b, other], part_recv.at[b], p_send_sem.at[b], p_recv_sem.at[b], other, chip)
+
+    my_quad = place // 4
+
+    def project_out(i, _):
+        b = (i // 4 + my_quad // 4) % 2
+        group = (my_quad + 4 - i % 4) % 4
+        first = b * HEADS + group * 4
+        for n in range(4):
+            pltpu.make_async_copy(o_recv.at[first + n], o_recv.at[first + n], o_recv_sem.at[first + n]).wait()
+        lhs = o_recv[pl.ds(first, 4)].reshape(256, TOK)
+        for side in range(2):
+            acc[b, side] += dot(lhs, wo_buf[group, :, side * 1024:(side + 1) * 1024], TN)
+
+        @pl.when(i % 4 == 3)
+        def _():
+            part_share(b).start()
+        return 0
+
+    lax.fori_loop(0, 8, project_out, 0)
+
+    def finish(n, _):
+        b = (n + my_quad // 4) % 2
         part_share(b).wait()
-        y_ref[b] = (mine_parts[b] + part_recv[b]).astype(BF16)
+        y_ref[b] = (acc[b, core] + part_recv[b]).astype(BF16)
+        return 0
+
+    lax.fori_loop(0, 2, finish, 0)
 
     @pl.when(mine)
     def _():
@@ -345,7 +362,7 @@
         x = hidden.reshape(2 * TOK, MODEL)
         wq = jnp.transpose(w_qk, (1, 2, 0)).reshape(HEADS * DIM, MODEL)
         wv = jnp.transpose(w_v, (1, 2, 0)).reshape(HEADS * DIM, MODEL)
-        wo = w_o.reshape(HEADS * DIM, MODEL)
+        wo = w_o.reshape(4, 256, MODEL)
         any_spec = pl.BlockSpec(memory_space=pl.ANY)
         vmem_spec = pl.BlockSpec(memory_space=pltpu.VMEM)
         dma = pltpu.SemaphoreType.DMA
@@ -357,7 +374,7 @@
             scratch_shapes=[
                 pltpu.VMEM((2 * TOK, MODEL), BF16),
                 pltpu.VMEM((4, 2, 256, MODEL), BF16),
-                pltpu.VMEM((HEADS * DIM, MODEL), BF16),
+                pltpu.VMEM((4, 256, MODEL), BF16),
                 pltpu.VMEM((HALF, 1, TOK), jnp.int32),
                 pltpu.VMEM((CHIPS, 1, TOK), jnp.int32),
                 pltpu.VMEM((HALF, 2 * DIM, TOK), BF16),
@@ -377,10 +394,10 @@
                 pltpu.VMEM((8, HALF // 2, 16, TOK), BF16),
                 pltpu.VMEM((HALF, DIM, TOK), BF16),
                 pltpu.VMEM((HALF, DIM, TOK), BF16),
+                pltpu.VMEM((2, 2, TOK, MODEL // 2), F32),
                 pltpu.VMEM((2, TOK, MODEL // 2), F32),
-                pltpu.VMEM((2, TOK, MODEL // 2), F32),
-                dma((10,)), dma(()), dma(()), dma(()), dma((HALF,)), dma((8,)), dma((8,)),
-                dma((4,)), dma((4,)), dma(()), dma(()), dma((2,)), dma((2,)),
+                dma((13,)), dma(()), dma(()), dma(()), dma((HALF,)), dma((8,)), dma((8,)),
+                dma((4,)), dma((4,)), dma(()), dma((HALF,)), dma((2,)), dma((2,)),
             ],
             compiler_params=pltpu.CompilerParams(collective_id=0, has_side_effects=True, vmem_limit_bytes=56 * 1024 * 1024),
             name="bucket_attention",

time: 64.2 us -> 60.4 us (0.941)
  Pallas kernels: 62.1 us -> 58.3 us
    pallas_call x1, Pallas kernels: 62.1 us -> 58.3 us  [step(): pl.pallas_call(kernel, out_shape=jax.ShapeDtypeStruct((2, TOK, MODEL // 2...]
where the time goes in v3:
time: 60.4 us; the launch traced here: 60.2 us
  Pallas kernels  58.3 us (97%)
  local copies, waits for them, and re-layouts  1.87 us (3%)
    pallas_call x1, Pallas kernels, step(): pl.pallas_call(kernel, out_shape=jax.ShapeDtypeStruct((2, TOK, MODEL // 2...  58.3 us
    unnamed x1, local copies, waits for them, and re-layouts  1.87 us

profile of v3, /device:TPU:1, one launch (start us, length us, event | category | flops | bytes accessed | tf_op | source)
XLA Modules:
  0.0 60.2 jit_solution(1125844859257340268)
XLA Ops:
  0.0 58.3 %bucket_attention.1 = bf16[2,128,1024]{2,1,0:T(8,128)(2,1)} custom-call(bf16[256,2048]{1,0:T(8,128)(2,1)} %bitcast.11, s32[2,16,128]{2,1,0:T(8,128)} %bucket_ref.1, bf16[1024,2048]{1,0:T(8,128)(2,1)} %bitcast.8, bf16[1024,2048]{1,0:T(8,128)(2,1)} %bitcast.9, bf16[4,256,2048]{2,1,0:T(8,128)(2,1)} %bitcast.10), custom_call_target="tpu_custom_call" | custom-call | tf_op jit(solution)/shard_map/bucket_attention/pallas_call | solution.py:369
  58.3 1.9 %copy.7 = bf16[2,128,1024]{2,1,0:T(8,128)(2,1)} copy(bf16[2,128,1024]{2,1,0:T(8,128)(2,1)} %bucket_attention.1) | data formatting | bytes 1048576

commit v4 on v3

--- a/solution.py
+++ b/solution.py
@@ -38,8 +38,8 @@
 def kernel(x_hbm, bucket_ref, wq_hbm, wv_hbm, wo_hbm, y_ref,
            x_buf, w_buf, wo_buf, b_send, b_recv, r_send, r_recv,
            first_rank, code_pair, code_quad, parity, slot_rank,
-           slots, slots_out, picks, keys, vals, qrows, back, back_out, o_send, o_recv, acc, part_recv,
-           load_sem, b_send_sem, b_recv_sem, r_send_sem, r_recv_sem, s_send_sem, s_recv_sem,
+           slots, slots_out, picks, token_hot, found_own, token_own, keys, vals, qrows, back, back_out, o_send, o_recv, acc, part_recv,
+           load_sem, b_send_sem, b_recv_sem, b_pass_sem, r_send_sem, r_recv_sem, s_send_sem, s_recv_sem,
            k_send_sem, k_recv_sem, o_send_sem, o_recv_sem, p_send_sem, p_recv_sem):
     core = lax.axis_index("tp")
     chip = lax.axis_index("sp")
@@ -74,14 +74,23 @@
 
     barrier = pltpu.get_barrier_semaphore()
 
-    def greet(s, _):
-        for t in range(2):
-            @pl.when((s != chip) | (core != t))
-            def _():
-                pl.semaphore_signal(barrier, inc=1, device_id=peer(t, s), device_id_type=pl.DeviceIdType.MESH)
-        return 0
-
-    lax.fori_loop(0, CHIPS, greet, 0)
+    def greet(t, s):
+        pl.semaphore_signal(barrier, inc=1, device_id=peer(t, s), device_id_type=pl.DeviceIdType.MESH)
+
+    def greet_chip(i, _):
+        spot = (place + i) % HALF
+        greet(0, core * HALF + spot)
+        greet(1, core * HALF + spot)
+        greet(half, other * HALF + spot)
+        return 0
+
+    lax.fori_loop(1, HALF, greet_chip, 0)
+    greet(half, other * HALF + place)
+    greet(1 - half, core * HALF + place)
+
+    @pl.when(jnp.logical_not(mine))
+    def _():
+        greet(half, core * HALF + place)
 
     for b in range(2):
         for h in range(HEADS):
@@ -123,20 +132,27 @@
         spot = (i + place) % HALF
         pair = (spot // HEADS) * HEADS + (spot % 4) * 4 + (spot // 4) % 4
         target = core * HALF + spot
-        for t in range(2):
-            @pl.when((target == chip) & (core == t))
-            def _():
-                pltpu.make_async_copy(b_send.at[pair], b_recv.at[chip], b_recv_sem).start()
-
-            @pl.when((target != chip) | (core != t))
-            def _():
-                remote(b_send.at[pair], b_recv.at[chip], b_send_sem, b_recv_sem, t, target).start()
+
+        @pl.when((i == 0) & mine)
+        def _():
+            pltpu.make_async_copy(b_send.at[pair], b_recv.at[chip], b_recv_sem).start()
+
+        @pl.when((i > 0) | jnp.logical_not(mine))
+        def _():
+            remote(b_send.at[pair], b_recv.at[chip], b_send_sem, b_recv_sem, half, target).start()
         return 0
 
     project(0)
     project(1)
     acc[...] = jnp.zeros_like(acc)
-    pl.semaphore_wait(barrier, 2 * CHIPS - 1)
+    @pl.when(mine)
+    def _():
+        pl.semaphore_wait(barrier, 95)
+
+    @pl.when(jnp.logical_not(mine))
+    def _():
+        pl.semaphore_wait(barrier, 96)
+
     lax.fori_loop(0, HALF, send_buckets, 0)
     send_rows(0)
     send_rows(1)
@@ -148,7 +164,11 @@
 
     lax.fori_loop(2, 4, project_more, 0)
 
-    pltpu.make_async_copy(b_recv, b_recv, b_recv_sem).wait()
+    own_rows = b_recv.at[pl.ds(core * HALF, HALF)]
+    pltpu.make_async_copy(own_rows, own_rows, b_recv_sem).wait()
+    bucket_share = remote(own_rows, own_rows, b_pass_sem.at[0], b_pass_sem.at[1], other, chip)
+    bucket_share.start()
+    bucket_share.wait()
     lane256 = iota((TOK, 256), 1)
     count_mat = one_hot((lane256 >= TOK) | (iota((TOK, 256), 0) < lane256))
     ids = iota((8, CHIPS, TOK), 1)
@@ -197,6 +217,25 @@
     slot_no = (iota((CHIPS, 256), 1) % SLOTS).astype(F32)
     slot_rank[...] = jnp.where(slot_no < filled, base + slot_no, -1.0)
 
+    rank_ids = iota((CHUNK, 256), 0).astype(F32)
+    ids_quad = iota((512, 512), 0).astype(F32)
+
+    def make_picks(i, _):
+        for a in range(11):
+            u = 11 * i + a
+            picks[u] = one_hot(slot_rank[pl.ds((u + CHIPS - 1) % CHIPS, 1), :] == rank_ids)
+        return 0
+
+    lax.fori_loop(0, (HALF + 1) // 11, make_picks, 0)
+
+    def make_hots(quad, _):
+        token = core * HALF + quad * 4
+        codes = jnp.concatenate([code_quad[token + a] for a in range(4)], axis=1)
+        token_hot[quad] = one_hot(codes == ids_quad)
+        return 0
+
+    lax.fori_loop(0, 8, make_hots, 0)
+
     owner_group = chip % 4
     ids512 = iota((512, 256), 0).astype(F32)
 
@@ -204,25 +243,36 @@
         return remote(slots_out.at[:, quad], slots.at[:, 8 + quad], s_send_sem.at[quad], s_recv_sem.at[quad], other, chip)
 
     def to_slots(i, _):
-        quad = 2 * ((owner_group + 8 - i // 2) % 4) + i % 2
+        octet = (owner_group + 4 - i) % 4
+        for n in range(8):
+            row = r_recv.at[octet * 8 + n]
+            pltpu.make_async_copy(row, row, r_recv_sem.at[octet * 8 + n]).wait()
         tiles = []
-        for a in range(2):
-            spot = quad * 4 + a * 2
-            for n in range(2):
-                pltpu.make_async_copy(r_recv.at[spot + n], r_recv.at[spot + n], r_recv_sem.at[spot + n]).wait()
+        for a in range(4):
+            spot = octet * 8 + a * 2
             token = core * HALF + spot
             codes = jnp.concatenate([code_pair[token], code_pair[token + 1]], axis=1)
             rows = jnp.concatenate([r_recv[spot], r_recv[spot + 1]], axis=1)
             tiles.append(dot(one_hot(codes == ids512), rows, NT).reshape(CHIPS, 8, TOK))
-        tile = jnp.concatenate(tiles, axis=1).astype(BF16)
-        slots[1:1 + HALF, quad] = tile[:HALF]
-        slots[0, quad] = tile[CHIPS - 1]
-        slots_out[1:1 + HALF, quad] = tile[HALF:]
-        slots_out[0, quad] = tile[HALF - 1]
-        share(quad).start()
-        return 0
-
-    lax.fori_loop(0, 8, to_slots, 0)
+        for r in range(2):
+            quad = 2 * octet + r
+            tile = jnp.concatenate(tiles[2 * r:2 * r + 2], axis=1).astype(BF16)
+            slots_out[1:1 + HALF, quad] = tile[HALF:]
+            slots_out[0, quad] = tile[HALF - 1]
+            share(quad).start()
+            slots[1:1 + HALF, quad] = tile[:HALF]
+            slots[0, quad] = tile[CHIPS - 1]
+        return 0
+
+    lax.fori_loop(0, 4, to_slots, 0)
+
+    def gather_own(i, _):
+        spots = [11 * i + a for a in range(11)]
+        for u in spots:
+            found_own[u] = dot(picks[u, :, :CHUNK], slots[u, :8].reshape(CHUNK, TOK)).astype(BF16)
+        return 0
+
+    lax.fori_loop(0, (HALF + 1) // 11, gather_own, 0)
 
     def share_wait(quad, _):
         share(quad).wait()
@@ -230,20 +280,18 @@
 
     lax.fori_loop(0, 8, share_wait, 0)
 
-    rank_ids = iota((CHUNK, 256), 0).astype(F32)
+    pick_vals = one_hot(iota((DIM, TOK), 0) + DIM == iota((DIM, TOK), 1))
 
     def gather_chunks(i, _):
         spots = [11 * i + a for a in range(11)]
-        chosen = [one_hot(slot_rank[pl.ds((u + CHIPS - 1) % CHIPS, 1), :] == rank_ids) for u in spots]
-        found = [dot(pick, slots[u].reshape(256, TOK)) for u, pick in zip(spots, chosen)]
-        for u, pick in zip(spots, chosen):
-            picks[u] = pick
+        found = [found_own[u].astype(F32) + dot(picks[u, :, CHUNK:], slots[u, 8:].reshape(CHUNK, TOK)) for u in spots]
         for u, rows in zip(spots, found):
             q_wide = rows[:, :DIM]
-            inverse = 1.0 / jnp.sqrt(jnp.sum(q_wide * q_wide, axis=1, keepdims=True))
+            inverse = lax.rsqrt(jnp.sum(q_wide * q_wide, axis=1, keepdims=True))
             keys[u] = (q_wide * inverse).astype(BF16)
-            qrows[u] = q_wide.astype(BF16)
-            vals[u] = rows[:, DIM:].T.astype(BF16)
+            narrow = rows.astype(BF16)
+            qrows[u] = narrow[:, :DIM]
+            vals[u] = dot(pick_vals, narrow, NT).astype(BF16)
         return 0
 
     lax.fori_loop(0, (HALF + 1) // 11, gather_chunks, 0)
@@ -278,44 +326,53 @@
 
     lax.fori_loop(0, HALF // 8, attend, 0)
 
+    def tokens_own(i, _):
+        for a in range(2):
+            quad = 2 * i + a
+            token_own[quad] = dot(back[quad, :16].reshape(256, TOK), token_hot[quad, :256], TN).astype(BF16)
+        return 0
+
+    lax.fori_loop(0, 4, tokens_own, 0)
+
     def back_wait(n, _):
         back_share(n).wait()
         return 0
 
     lax.fori_loop(0, 4, back_wait, 0)
 
-    ids_quad = iota((512, 512), 0).astype(F32)
     my_batch = place // HEADS
     my_pair = my_batch * HEADS + (chip % 4) * 4 + (chip // 4) % 4
 
     def to_tokens(i, _):
-        quad = (((i // 4) + my_batch) % 2) * 4 + (i + chip) % 4
-        token = core * HALF + quad * 4
-        codes = jnp.concatenate([code_quad[token + a] for a in range(4)], axis=1)
-        odd = jnp.concatenate([parity[token + a] for a in range(4)], axis=1)
-        both = dot(back[quad].reshape(512, TOK), one_hot(codes == ids_quad), TN)
-        rows = jnp.where(odd > 0.5, both[DIM:], both[:DIM]).astype(BF16)
-        for a in range(4):
-            o_send[quad * 4 + a] = rows[:, a * TOK:(a + 1) * TOK]
-        for n in range(4):
-            a = (n + chip // 4 + chip // 16) % 4
-            target = token + a
-
-            @pl.when((target == chip) & mine)
-            def _():
-                pltpu.make_async_copy(o_send.at[quad * 4 + a], o_recv.at[my_pair], o_recv_sem.at[my_pair]).start()
-
-            @pl.when((target != chip) | jnp.logical_not(mine))
-            def _():
-                remote(o_send.at[quad * 4 + a], o_recv.at[my_pair], o_send_sem, o_recv_sem.at[my_pair], half, target).start()
-        return 0
-
-    lax.fori_loop(0, 8, to_tokens, 0)
+        quads = [((i // 2 + my_batch) % 2) * 4 + (2 * i + m + chip) % 4 for m in range(2)]
+        late = [dot(back[quad, 16:].reshape(256, TOK), token_hot[quad, 256:], TN) for quad in quads]
+        for quad, part in zip(quads, late):
+            token = core * HALF + quad * 4
+            odd = jnp.concatenate([parity[token + a] for a in range(4)], axis=1)
+            both = part + token_own[quad].astype(F32)
+            rows = jnp.where(odd > 0.5, both[DIM:], both[:DIM]).astype(BF16)
+            for a in range(4):
+                o_send[quad * 4 + a] = rows[:, a * TOK:(a + 1) * TOK]
+        for quad in quads:
+            for n in range(4):
+                a = (n + chip // 4 + chip // 16) % 4
+                target = core * HALF + quad * 4 + a
+
+                @pl.when((target == chip) & mine)
+                def _():
+                    pltpu.make_async_copy(o_send.at[quad * 4 + a], o_recv.at[my_pair], o_recv_sem.at[my_pair]).start()
+
+                @pl.when((target != chip) | jnp.logical_not(mine))
+                def _():
+                    remote(o_send.at[quad * 4 + a], o_recv.at[my_pair], o_send_sem, o_recv_sem.at[my_pair], half, target).start()
+        return 0
+
+    lax.fori_loop(0, 4, to_tokens, 0)
     for load in wo_loads:
         load.wait()
 
-    def part_share(b):
-        return remote(acc.at[b, other], part_recv.at[b], p_send_sem.at[b], p_recv_sem.at[b], other, chip)
+    def part_share(b, n):
+        return remote(acc.at[b, other, n], part_recv.at[b, n], p_send_sem.at[b, n], p_recv_sem.at[b, n], other, chip)
 
     my_quad = place // 4
 
@@ -324,35 +381,38 @@
         group = (my_quad + 4 - i % 4) % 4
         first = b * HEADS + group * 4
         for n in range(4):
-            pltpu.make_async_copy(o_recv.at[first + n], o_recv.at[first + n], o_recv_sem.at[first + n]).wait()
+            row = o_recv.at[first + n]
+            pltpu.make_async_copy(row, row, o_recv_sem.at[first + n]).wait()
         lhs = o_recv[pl.ds(first, 4)].reshape(256, TOK)
-        for side in range(2):
-            acc[b, side] += dot(lhs, wo_buf[group, :, side * 1024:(side + 1) * 1024], TN)
-
-        @pl.when(i % 4 == 3)
-        def _():
-            part_share(b).start()
+        for side in (other, core):
+            for n in range(2):
+                acc[b, side, n] += dot(lhs, wo_buf[group, :, pl.ds(pl.multiple_of(side * 1024 + n * 512, 512), 512)], TN)
+                if side is other:
+                    @pl.when(i % 4 == 3)
+                    def _():
+                        part_share(b, n).start()
         return 0
 
     lax.fori_loop(0, 8, project_out, 0)
 
-    def finish(n, _):
-        b = (n + my_quad // 4) % 2
-        part_share(b).wait()
-        y_ref[b] = (acc[b, core] + part_recv[b]).astype(BF16)
+    def finish(i, _):
+        b = (i + my_quad // 4) % 2
+        for n in range(2):
+            part_share(b, n).wait()
+            y_ref[b, :, n * 512:(n + 1) * 512] = (acc[b, core, n] + part_recv[b, n]).astype(BF16)
         return 0
 
     lax.fori_loop(0, 2, finish, 0)
 
     @pl.when(mine)
     def _():
-        pltpu.make_async_copy(b_recv.at[0:63], b_recv.at[0:63], b_send_sem).wait()
+        pltpu.make_async_copy(b_send.at[0:31], b_send.at[0:31], b_send_sem).wait()
         pltpu.make_async_copy(r_send.at[0:31], r_send.at[0:31], r_send_sem).wait()
         pltpu.make_async_copy(o_send.at[0:31], o_send.at[0:31], o_send_sem).wait()
 
     @pl.when(jnp.logical_not(mine))
     def _():
-        pltpu.make_async_copy(b_recv, b_recv, b_send_sem).wait()
+        pltpu.make_async_copy(b_send, b_send, b_send_sem).wait()
         pltpu.make_async_copy(r_send, r_send, r_send_sem).wait()
         pltpu.make_async_copy(o_send, o_send, o_send_sem).wait()
 
@@ -368,7 +428,7 @@
         dma = pltpu.SemaphoreType.DMA
         return pl.pallas_call(
             kernel,
-            out_shape=jax.ShapeDtypeStruct((2, TOK, MODEL // 2), BF16),
+            out_shape=pltpu.VMEM((2, TOK, MODEL // 2), BF16),
             in_specs=[any_spec, vmem_spec, any_spec, any_spec, any_spec],
             out_specs=vmem_spec,
             scratch_shapes=[
@@ -387,6 +447,9 @@
                 pltpu.VMEM((HALF + 1, 16, 16, TOK), BF16),
                 pltpu.VMEM((HALF + 1, 8, 16, TOK), BF16),
                 pltpu.VMEM((HALF + 1, CHUNK, 256), BF16),
+                pltpu.VMEM((8, 512, 512), BF16),
+                pltpu.VMEM((HALF + 1, CHUNK, TOK), BF16),
+                pltpu.VMEM((8, TOK, 512), BF16),
                 pltpu.VMEM((HALF + 1, CHUNK, DIM), BF16),
                 pltpu.VMEM((HALF + 1, DIM, CHUNK), BF16),
                 pltpu.VMEM((HALF + 1, CHUNK, DIM), BF16),
@@ -394,10 +457,10 @@
                 pltpu.VMEM((8, HALF // 2, 16, TOK), BF16),
                 pltpu.VMEM((HALF, DIM, TOK), BF16),
                 pltpu.VMEM((HALF, DIM, TOK), BF16),
-                pltpu.VMEM((2, 2, TOK, MODEL // 2), F32),
-                pltpu.VMEM((2, TOK, MODEL // 2), F32),
-                dma((13,)), dma(()), dma(()), dma(()), dma((HALF,)), dma((8,)), dma((8,)),
-                dma((4,)), dma((4,)), dma(()), dma((HALF,)), dma((2,)), dma((2,)),
+                pltpu.VMEM((2, 2, 2, TOK, 512), F32),
+                pltpu.VMEM((2, 2, TOK, 512), F32),
+                dma((13,)), dma(()), dma(()), dma((2,)), dma(()), dma((HALF,)), dma((8,)), dma((8,)),
+                dma((4,)), dma((4,)), dma(()), dma((HALF,)), dma((2, 2)), dma((2, 2)),
             ],
             compiler_params=pltpu.CompilerParams(collective_id=0, has_side_effects=True, vmem_limit_bytes=56 * 1024 * 1024),
             name="bucket_attention",

time: 60.4 us -> 56.2 us (0.930)
  Pallas kernels: 58.3 us -> 55.3 us
  local copies, waits for them, and re-layouts: 1.87 us -> 0.8 us
    pallas_call x1, Pallas kernels: 58.3 us -> 55.3 us  [step(): pl.pallas_call(kernel, out_shape=pltpu.VMEM((2, TOK, MODEL // 2), BF16),...]
    unnamed x1, local copies, waits for them, and re-layouts: 1.87 us -> 0.8 us
where the time goes in v4:
time: 56.2 us; the launch traced here: 56.1 us
  Pallas kernels  55.3 us (98%)
  local copies, waits for them, and re-layouts  0.8 us (1%)
    pallas_call x1, Pallas kernels, step(): pl.pallas_call(kernel, out_shape=pltpu.VMEM((2, TOK, MODEL // 2), BF16),...  55.3 us

profile of v4, /device:TPU:1, one launch (start us, length us, event | category | flops | bytes accessed | tf_op | source)
XLA Modules:
  0.0 56.1 jit_solution(15502211734541239785)
XLA Ops:
  0.0 55.3 %bucket_attention.1 = bf16[2,128,1024]{2,1,0:T(8,128)(2,1)S(1)} custom-call(bf16[256,2048]{1,0:T(8,128)(2,1)} %bitcast.11, s32[2,16,128]{2,1,0:T(8,128)} %bucket_ref.1, bf16[1024,2048]{1,0:T(8,128)(2,1)} %bitcast.8, bf16[1024,2048]{1,0:T(8,128)(2,1)} %bitcast.9, bf16[4,256,2048]{2,1,0:T(8,128)(2,1)} %bitcast.10), custom_call_target="tpu_custom_call" | custom-call | tf_op jit(solution)/shard_map/bucket_attention/pallas_call | solution.py:429
  55.3 0.8 %copy.7 = bf16[2,128,1024]{2,1,0:T(8,128)(2,1)} copy(bf16[2,128,1024]{2,1,0:T(8,128)(2,1)S(1)} %bucket_attention.1) | data formatting | bytes 1048576

commit v5 on v4

--- a/solution.py
+++ b/solution.py
@@ -15,6 +15,7 @@
 DIM = 64
 MODEL = 2048
 SLOTS = 4
+SPAN = 32
 MASKED = -8e5
 EXP_SCALE = 0.125 * 1.4426950408889634
 F32 = jnp.float32
@@ -143,7 +144,6 @@
         return 0
 
     project(0)
-    project(1)
     acc[...] = jnp.zeros_like(acc)
     @pl.when(mine)
     def _():
@@ -155,14 +155,13 @@
 
     lax.fori_loop(0, HALF, send_buckets, 0)
     send_rows(0)
-    send_rows(1)
 
     def project_more(step, _):
         project(step)
         send_rows(step)
         return 0
 
-    lax.fori_loop(2, 4, project_more, 0)
+    lax.fori_loop(1, 4, project_more, 0)
 
     own_rows = b_recv.at[pl.ds(core * HALF, HALF)]
     pltpu.make_async_copy(own_rows, own_rows, b_recv_sem).wait()
@@ -171,45 +170,45 @@
     bucket_share.wait()
     lane256 = iota((TOK, 256), 1)
     count_mat = one_hot((lane256 >= TOK) | (iota((TOK, 256), 0) < lane256))
-    ids = iota((8, CHIPS, TOK), 1)
+    ids = iota((SPAN, CHIPS, TOK), 1)
     ids_f = ids.astype(F32)
 
     def rank_first(i, running):
-        hot = jnp.where(b_recv[pl.ds(8 * i, 8)] == ids, 1.0, 0.0)
-        counts = dot(hot.astype(BF16).reshape(512, TOK), count_mat)
-        for a in range(8):
+        hot = jnp.where(b_recv[pl.ds(SPAN * i, SPAN)] == ids, 1.0, 0.0)
+        counts = dot(hot.astype(BF16).reshape(SPAN * CHIPS, TOK), count_mat)
+        for a in range(SPAN):
             block = counts[a * CHIPS:(a + 1) * CHIPS]
-            first_rank[8 * i + a] = jnp.sum(hot[a] * (block[:, :TOK] + running), axis=0, keepdims=True)
+            first_rank[SPAN * i + a] = jnp.sum(hot[a] * (block[:, :TOK] + running), axis=0, keepdims=True)
             running = running + block[:, TOK:]
         return running
 
-    totals = lax.fori_loop(0, 8, rank_first, jnp.zeros((CHIPS, TOK), F32))
+    totals = lax.fori_loop(0, CHIPS // SPAN, rank_first, jnp.zeros((CHIPS, TOK), F32))
     high = jnp.floor(totals * (1.0 / 64))
     low = totals - 64.0 * high
     below = one_hot(iota((CHIPS, CHIPS), 1) < iota((CHIPS, CHIPS), 0))
     offsets = 64.0 * dot(below, high.astype(BF16)) + dot(below, low.astype(BF16))
     shift = (core * HALF).astype(F32)
-    within = iota((8, 1, TOK), 0)
+    within = iota((SPAN, 1, TOK), 0)
     lane_id = iota((CHIPS, TOK), 1)
 
     def rank_second(i, chunk_counts):
-        hot = jnp.where(b_recv[pl.ds(8 * i, 8)] == ids, 1.0, 0.0)
-        rank = first_rank[pl.ds(8 * i, 8)] + jnp.sum(hot * offsets[None], axis=1, keepdims=True)
+        hot = jnp.where(b_recv[pl.ds(SPAN * i, SPAN)] == ids, 1.0, 0.0)
+        rank = first_rank[pl.ds(SPAN * i, SPAN)] + jnp.sum(hot * offsets[None], axis=1, keepdims=True)
         chunk = jnp.floor(rank * (1.0 / CHUNK)) - shift
         chunk = jnp.where(chunk < 0.0, chunk + float(CHIPS), chunk)
         hot = jnp.where(chunk == ids_f, 1.0, 0.0)
-        counts = dot(hot.astype(BF16).reshape(512, TOK), count_mat)
-        slot = jnp.sum(hot * counts[:, :TOK].reshape(8, CHIPS, TOK), axis=1, keepdims=True)
+        counts = dot(hot.astype(BF16).reshape(SPAN * CHIPS, TOK), count_mat)
+        slot = jnp.sum(hot * counts[:, :TOK].reshape(SPAN, CHIPS, TOK), axis=1, keepdims=True)
         two = jnp.floor(chunk * 0.5)
-        code_pair[pl.ds(8 * i, 8)] = chunk * 8.0 + slot + ((within % 2) * SLOTS).astype(F32)
-        code_quad[pl.ds(8 * i, 8)] = two * 16.0 + slot + ((within % 4) * SLOTS).astype(F32)
-        parity[pl.ds(8 * i, 8)] = chunk - 2.0 * two
-        for a in range(8):
-            spot = (8 * i + a + core * HALF) % CHIPS
+        code_pair[pl.ds(SPAN * i, SPAN)] = chunk * 8.0 + slot + ((within % 2) * SLOTS).astype(F32)
+        code_quad[pl.ds(SPAN * i, SPAN)] = two * 16.0 + slot + ((within % 4) * SLOTS).astype(F32)
+        parity[pl.ds(SPAN * i, SPAN)] = chunk - 2.0 * two
+        for a in range(SPAN):
+            spot = (SPAN * i + a + core * HALF) % CHIPS
             chunk_counts = chunk_counts + jnp.where(lane_id == spot, counts[a * CHIPS:(a + 1) * CHIPS, TOK:], 0.0)
         return chunk_counts
 
-    chunk_counts = lax.fori_loop(0, 8, rank_second, jnp.zeros((CHIPS, TOK), F32)).astype(BF16)
+    chunk_counts = lax.fori_loop(0, CHIPS // SPAN, rank_second, jnp.zeros((CHIPS, TOK), F32)).astype(BF16)
     source = iota((TOK, 256), 1) // SLOTS
     sources = iota((TOK, 256), 0)
     base = dot(chunk_counts, one_hot(sources < source))
@@ -267,12 +266,12 @@
     lax.fori_loop(0, 4, to_slots, 0)
 
     def gather_own(i, _):
-        spots = [11 * i + a for a in range(11)]
+        spots = [33 * i + a for a in range(33)]
         for u in spots:
             found_own[u] = dot(picks[u, :, :CHUNK], slots[u, :8].reshape(CHUNK, TOK)).astype(BF16)
         return 0
 
-    lax.fori_loop(0, (HALF + 1) // 11, gather_own, 0)
+    lax.fori_loop(0, (HALF + 1) // 33, gather_own, 0)
 
     def share_wait(quad, _):
         share(quad).wait()
@@ -283,7 +282,7 @@
     pick_vals = one_hot(iota((DIM, TOK), 0) + DIM == iota((DIM, TOK), 1))
 
     def gather_chunks(i, _):
-        spots = [11 * i + a for a in range(11)]
+        spots = [33 * i + a for a in range(33)]
         found = [found_own[u].astype(F32) + dot(picks[u, :, CHUNK:], slots[u, 8:].reshape(CHUNK, TOK)) for u in spots]
         for u, rows in zip(spots, found):
             q_wide = rows[:, :DIM]
@@ -294,7 +293,7 @@
             vals[u] = dot(pick_vals, narrow, NT).astype(BF16)
         return 0
 
-    lax.fori_loop(0, (HALF + 1) // 11, gather_chunks, 0)
+    lax.fori_loop(0, (HALF + 1) // 33, gather_chunks, 0)
     diagonal = iota((CHUNK, CHUNK), 0) == iota((CHUNK, CHUNK), 1)
 
     def back_share(n):
@@ -311,28 +310,29 @@
         return jnp.concatenate([(before * inverse).astype(BF16), (now * inverse).astype(BF16)], axis=0)
 
     def attend(n, _):
-        spots = [8 * n + a + 1 for a in range(8)]
+        spots = [32 * n + a + 1 for a in range(32)]
         scores = [dot(keys[pl.ds(u - 1, 2)].reshape(2 * CHUNK, DIM), qrows[u], NT) for u in spots]
         probs = [softmax(both) for both in scores]
         outs = [dot(jnp.concatenate([vals[u - 1], vals[u]], axis=1), p).astype(BF16) for u, p in zip(spots, probs)]
         spread = [dot(o, picks[u]) for u, o in zip(spots, outs)]
-        for m in range(4):
+        for m in range(16):
             tile = jnp.concatenate(spread[2 * m:2 * m + 2], axis=0).T.astype(BF16).reshape(16, 16, TOK)
-            back[:, 4 * n + m] = tile[:8]
-            back_out[:, 4 * n + m] = tile[8:]
-
-        back_share(n).start()
-        return 0
-
-    lax.fori_loop(0, HALF // 8, attend, 0)
+            back[:, 16 * n + m] = tile[:8]
+            back_out[:, 16 * n + m] = tile[8:]
+
+        for part in range(4):
+            back_share(part).start()
+        return 0
+
+    lax.fori_loop(0, HALF // 32, attend, 0)
 
     def tokens_own(i, _):
-        for a in range(2):
-            quad = 2 * i + a
+        for a in range(4):
+            quad = 4 * i + a
             token_own[quad] = dot(back[quad, :16].reshape(256, TOK), token_hot[quad, :256], TN).astype(BF16)
         return 0
 
-    lax.fori_loop(0, 4, tokens_own, 0)
+    lax.fori_loop(0, 2, tokens_own, 0)
 
     def back_wait(n, _):
         back_share(n).wait()
@@ -355,7 +355,7 @@
                 o_send[quad * 4 + a] = rows[:, a * TOK:(a + 1) * TOK]
         for quad in quads:
             for n in range(4):
-                a = (n + chip // 4 + chip // 16) % 4
+                a = (n + chip + chip // 4 + chip // 16) % 4
                 target = core * HALF + quad * 4 + a
 
                 @pl.when((target == chip) & mine)

time: 56.2 us -> 52.8 us (0.940)
  Pallas kernels: 55.3 us -> 51.8 us
    pallas_call x1, Pallas kernels: 55.3 us -> 51.8 us  [step(): pl.pallas_call(kernel, out_shape=pltpu.VMEM((2, TOK, MODEL // 2), BF16),...]
where the time goes in v5:
time: 52.8 us; the launch traced here: 52.6 us
  Pallas kernels  51.8 us (98%)
  local copies, waits for them, and re-layouts  0.8 us (2%)
    pallas_call x1, Pallas kernels, step(): pl.pallas_call(kernel, out_shape=pltpu.VMEM((2, TOK, MODEL // 2), BF16),...  51.8 us

profile of v5, /device:TPU:1, one launch (start us, length us, event | category | flops | bytes accessed | tf_op | source)
XLA Modules:
  0.0 52.6 jit_solution(17741404729189866579)
XLA Ops:
  0.0 51.8 %bucket_attention.1 = bf16[2,128,1024]{2,1,0:T(8,128)(2,1)S(1)} custom-call(bf16[256,2048]{1,0:T(8,128)(2,1)} %bitcast.11, s32[2,16,128]{2,1,0:T(8,128)} %bucket_ref.1, bf16[1024,2048]{1,0:T(8,128)(2,1)} %bitcast.8, bf16[1024,2048]{1,0:T(8,128)(2,1)} %bitcast.9, bf16[4,256,2048]{2,1,0:T(8,128)(2,1)} %bitcast.10), custom_call_target="tpu_custom_call" | custom-call | tf_op jit(solution)/shard_map/bucket_attention/pallas_call | solution.py:429
  51.8 0.8 %copy.7 = bf16[2,128,1024]{2,1,0:T(8,128)(2,1)} copy(bf16[2,128,1024]{2,1,0:T(8,128)(2,1)S(1)} %bucket_attention.1) | data formatting | bytes 1048576

commit v6 on v5

--- a/solution.py
+++ b/solution.py
@@ -39,9 +39,9 @@
 def kernel(x_hbm, bucket_ref, wq_hbm, wv_hbm, wo_hbm, y_ref,
            x_buf, w_buf, wo_buf, b_send, b_recv, r_send, r_recv,
            first_rank, code_pair, code_quad, parity, slot_rank,
-           slots, slots_out, picks, token_hot, found_own, token_own, keys, vals, qrows, back, back_out, o_send, o_recv, acc, part_recv,
+           slots, slots_out, picks, token_hot, found_own, token_own, keys, vals, qrows, back, back_out, o_send, o_recv, o_far, wo_far, acc,
            load_sem, b_send_sem, b_recv_sem, b_pass_sem, r_send_sem, r_recv_sem, s_send_sem, s_recv_sem,
-           k_send_sem, k_recv_sem, o_send_sem, o_recv_sem, p_send_sem, p_recv_sem):
+           k_send_sem, k_recv_sem, o_send_sem, o_recv_sem, p_send_sem, p_recv_sem, w_pass_sem):
     core = lax.axis_index("tp")
     chip = lax.axis_index("sp")
     other = 1 - core
@@ -114,7 +114,7 @@
         group = (step + turn) % 4
 
         def body(i, _):
-            spot = (i + chip // 4 + chip // 16) % 8
+            spot = (chip // 4 + chip // 16 + 8 - i) % 8
             pair = (spot // 4) * HEADS + group * 4 + spot % 4
             target = core * HALF + (spot // 4) * HEADS + (spot % 4) * 4 + group
 
@@ -162,6 +162,13 @@
         return 0
 
     lax.fori_loop(1, 4, project_more, 0)
+
+    for load in wo_loads:
+        load.wait()
+    my_columns = pl.ds(pl.multiple_of(core * 1024, 1024), 1024)
+    wo_share = remote(wo_buf.at[:, :, pl.ds(pl.multiple_of(other * 1024, 1024), 1024)], wo_far,
+                      w_pass_sem.at[0], w_pass_sem.at[1], other, chip)
+    wo_share.start()
 
     own_rows = b_recv.at[pl.ds(core * HALF, HALF)]
     pltpu.make_async_copy(own_rows, own_rows, b_recv_sem).wait()
@@ -368,41 +375,41 @@
         return 0
 
     lax.fori_loop(0, 4, to_tokens, 0)
-    for load in wo_loads:
-        load.wait()
-
-    def part_share(b, n):
-        return remote(acc.at[b, other, n], part_recv.at[b, n], p_send_sem.at[b, n], p_recv_sem.at[b, n], other, chip)
-
     my_quad = place // 4
 
+    def arrival(i):
+        batch = (i // 4 + my_quad // 4) % 2
+        group = (my_quad + 4 - i % 4) % 4
+        return batch, group, batch * HEADS + group * 4
+
+    def pass_rows(i):
+        rows = pl.ds(arrival(i)[2], 4)
+        return remote(o_recv.at[rows], o_far.at[rows], p_send_sem.at[i], p_recv_sem.at[i], other, chip)
+
+    def far_product(i):
+        batch, group, first = arrival(i)
+        pass_rows(i).wait()
+        return dot(o_far[pl.ds(first, 4)].reshape(256, TOK), wo_far[group], TN)
+
+    wo_share.wait()
+
     def project_out(i, _):
-        b = (i // 4 + my_quad // 4) % 2
-        group = (my_quad + 4 - i % 4) % 4
-        first = b * HEADS + group * 4
+        batch, group, first = arrival(i)
         for n in range(4):
             row = o_recv.at[first + n]
             pltpu.make_async_copy(row, row, o_recv_sem.at[first + n]).wait()
-        lhs = o_recv[pl.ds(first, 4)].reshape(256, TOK)
-        for side in (other, core):
-            for n in range(2):
-                acc[b, side, n] += dot(lhs, wo_buf[group, :, pl.ds(pl.multiple_of(side * 1024 + n * 512, 512), 512)], TN)
-                if side is other:
-                    @pl.when(i % 4 == 3)
-                    def _():
-                        part_share(b, n).start()
+        pass_rows(i).start()
+        acc[batch] += dot(o_recv[pl.ds(first, 4)].reshape(256, TOK), wo_buf[group, :, my_columns], TN)
+
+        @pl.when(i > 0)
+        def _():
+            acc[arrival(i - 1)[0]] += far_product(i - 1)
         return 0
 
     lax.fori_loop(0, 8, project_out, 0)
-
-    def finish(i, _):
-        b = (i + my_quad // 4) % 2
-        for n in range(2):
-            part_share(b, n).wait()
-            y_ref[b, :, n * 512:(n + 1) * 512] = (acc[b, core, n] + part_recv[b, n]).astype(BF16)
-        return 0
-
-    lax.fori_loop(0, 2, finish, 0)
+    last = arrival(7)[0]
+    y_ref[1 - last] = acc[1 - last].astype(BF16)
+    y_ref[last] = (acc[last] + far_product(7)).astype(BF16)
 
     @pl.when(mine)
     def _():
@@ -457,10 +464,11 @@
                 pltpu.VMEM((8, HALF // 2, 16, TOK), BF16),
                 pltpu.VMEM((HALF, DIM, TOK), BF16),
                 pltpu.VMEM((HALF, DIM, TOK), BF16),
-                pltpu.VMEM((2, 2, 2, TOK, 512), F32),
-                pltpu.VMEM((2, 2, TOK, 512), F32),
+                pltpu.VMEM((HALF, DIM, TOK), BF16),
+                pltpu.VMEM((4, 256, 1024), BF16),
+                pltpu.VMEM((2, TOK, 1024), F32),
                 dma((13,)), dma(()), dma(()), dma((2,)), dma(()), dma((HALF,)), dma((8,)), dma((8,)),
-                dma((4,)), dma((4,)), dma(()), dma((HALF,)), dma((2, 2)), dma((2, 2)),
+                dma((4,)), dma((4,)), dma(()), dma((HALF,)), dma((8,)), dma((8,)), dma((2,)),
             ],
             compiler_params=pltpu.CompilerParams(collective_id=0, has_side_effects=True, vmem_limit_bytes=56 * 1024 * 1024),
             name="bucket_attention",

time: 52.8 us -> 52.7 us (level)
  no operation moved by 1% of the time
where the time goes in v6:
time: 52.7 us; the launch traced here: 52.4 us
  Pallas kernels  51.6 us (98%)
  local copies, waits for them, and re-layouts  0.8 us (2%)
    pallas_call x1, Pallas kernels, step(): pl.pallas_call(kernel, out_shape=pltpu.VMEM((2, TOK, MODEL // 2), BF16),...  51.6 us

profile of v6, /device:TPU:1, one launch (start us, length us, event | category | flops | bytes accessed | tf_op | source)
XLA Modules:
  0.0 52.4 jit_solution(286640421840333568)
XLA Ops:
  0.0 51.6 %bucket_attention.1 = bf16[2,128,1024]{2,1,0:T(8,128)(2,1)S(1)} custom-call(bf16[256,2048]{1,0:T(8,128)(2,1)} %bitcast.11, s32[2,16,128]{2,1,0:T(8,128)} %bucket_ref.1, bf16[1024,2048]{1,0:T(8,128)(2,1)} %bitcast.8, bf16[1024,2048]{1,0:T(8,128)(2,1)} %bitcast.9, bf16[4,256,2048]{2,1,0:T(8,128)(2,1)} %bitcast.10), custom_call_target="tpu_custom_call" | custom-call | tf_op jit(solution)/shard_map/bucket_attention/pallas_call | solution.py:436
  51.6 0.8 %copy.7 = bf16[2,128,1024]{2,1,0:T(8,128)(2,1)} copy(bf16[2,128,1024]{2,1,0:T(8,128)(2,1)S(1)} %bucket_attention.1) | data formatting | bytes 1048576

commit v7 on v6

--- a/solution.py
+++ b/solution.py
@@ -233,14 +233,6 @@
         return 0
 
     lax.fori_loop(0, (HALF + 1) // 11, make_picks, 0)
-
-    def make_hots(quad, _):
-        token = core * HALF + quad * 4
-        codes = jnp.concatenate([code_quad[token + a] for a in range(4)], axis=1)
-        token_hot[quad] = one_hot(codes == ids_quad)
-        return 0
-
-    lax.fori_loop(0, 8, make_hots, 0)
 
     owner_group = chip % 4
     ids512 = iota((512, 256), 0).astype(F32)
@@ -279,6 +271,14 @@
         return 0
 
     lax.fori_loop(0, (HALF + 1) // 33, gather_own, 0)
+
+    def make_hots(quad, _):
+        token = core * HALF + quad * 4
+        codes = jnp.concatenate([code_quad[token + a] for a in range(4)], axis=1)
+        token_hot[quad] = one_hot(codes == ids_quad)
+        return 0
+
+    lax.fori_loop(0, 8, make_hots, 0)
 
     def share_wait(quad, _):
         share(quad).wait()

time: 52.7 us -> 54.4 us (1.032)
  Pallas kernels: 51.6 us -> 53.4 us
    pallas_call x1, Pallas kernels: 51.6 us -> 53.4 us  [step(): pl.pallas_call(kernel, out_shape=pltpu.VMEM((2, TOK, MODEL // 2), BF16),...]
where the time goes in v7:
time: 54.4 us; the launch traced here: 54.2 us
  Pallas kernels  53.4 us (98%)
  local copies, waits for them, and re-layouts  0.8 us (1%)
    pallas_call x1, Pallas kernels, step(): pl.pallas_call(kernel, out_shape=pltpu.VMEM((2, TOK, MODEL // 2), BF16),...  53.4 us

profile of v7, /device:TPU:1, one launch (start us, length us, event | category | flops | bytes accessed | tf_op | source)
XLA Modules:
  0.0 54.2 jit_solution(4543443294032555457)
XLA Ops:
  0.0 53.4 %bucket_attention.1 = bf16[2,128,1024]{2,1,0:T(8,128)(2,1)S(1)} custom-call(bf16[256,2048]{1,0:T(8,128)(2,1)} %bitcast.11, s32[2,16,128]{2,1,0:T(8,128)} %bucket_ref.1, bf16[1024,2048]{1,0:T(8,128)(2,1)} %bitcast.8, bf16[1024,2048]{1,0:T(8,128)(2,1)} %bitcast.9, bf16[4,256,2048]{2,1,0:T(8,128)(2,1)} %bitcast.10), custom_call_target="tpu_custom_call" | custom-call | tf_op jit(solution)/shard_map/bucket_attention/pallas_call | solution.py:436
  53.4 0.8 %copy.7 = bf16[2,128,1024]{2,1,0:T(8,128)(2,1)} copy(bf16[2,128,1024]{2,1,0:T(8,128)(2,1)S(1)} %bucket_attention.1) | data formatting | bytes 1048576
